TPU v7x, 32 devices: a 4x4x1 block of a 4x4x8 slice. The times are simulated.
32 devices in a mesh: dp: 1 (over z), fsdp: 4 (over y), tp: 8 (over x, core).
Axes of the slice: x: 4, y: 4, z: 1, core: 2. Of those that a mesh axis runs over, the one named last changes fastest.
The devices are a block of a 4x4x8 slice.
Arguments:
- hidden: bfloat16 [16384, 1024], P(('dp', 'fsdp', 'tp'))
- w_head: bfloat16 [1024, 50304], P('fsdp', 'tp')
- labels: int32 [16384], P(('dp', 'fsdp', 'tp'))
Outputs:
- output 1: float32 [1], P('dp')
- output 2: bfloat16 [16384, 1024], P(('dp', 'fsdp', 'tp'))
- output 3: bfloat16 [1024, 50304], P(('dp', 'fsdp'), 'tp')
All inputs are finite; a program needn't handle non-finite values.
Results may differ from a plain program's by a relative error of at most 0.001.
Values are sent between devices in bfloat16 or wider.
A program may use at most 768 MiB of HBM per device.

v0:
```python
import jax
import jax.numpy as jnp
from jax import lax
from jax.sharding import PartitionSpec as P


def solution(mesh):
    fsdp_size = mesh.shape["fsdp"]
    tp_size = mesh.shape["tp"]
    token_spec = P(("dp", "fsdp", "tp"), None)
    label_spec = P(("dp", "fsdp", "tp"))

    def local_step(hidden, w_head, labels):
        rows_dev = hidden.shape[0]
        vocab_dev = w_head.shape[1]
        inv_tokens = 1.0 / (rows_dev * tp_size * fsdp_size)
        w_full = lax.all_gather(w_head, "fsdp", axis=0, tiled=True)
        x_full = lax.all_gather(hidden, "tp", axis=0, tiled=True)
        lab_full = lax.all_gather(labels, "tp", axis=0, tiled=True)
        logits = jnp.dot(x_full, w_full, preferred_element_type=jnp.float32)
        row_max = lax.pmax(jnp.max(logits, axis=1), "tp")
        exp_rows = jnp.exp(logits - row_max[:, None])
        local_ids = lab_full - lax.axis_index("tp") * vocab_dev
        onehot = local_ids[:, None] == jnp.arange(vocab_dev, dtype=jnp.int32)[None, :]
        local_stats = jnp.stack([jnp.sum(exp_rows, axis=1), jnp.sum(jnp.where(onehot, logits, 0.0), axis=1)])
        stat_sums = lax.psum(local_stats, "tp")
        row_sum = stat_sums[0]
        target = stat_sums[1]
        tok_loss = row_max + jnp.log(row_sum) - target
        mean_loss = lax.psum(jnp.sum(tok_loss), "fsdp") * inv_tokens
        prob_rows = exp_rows / row_sum[:, None]
        grad_logits = (jnp.where(onehot, prob_rows - 1.0, prob_rows) * inv_tokens).astype(jnp.bfloat16)
        d_x_part = jnp.einsum("tv,hv->th", grad_logits, w_full, preferred_element_type=jnp.float32)
        d_hidden = lax.psum_scatter(d_x_part, "tp", scatter_dimension=0, tiled=True).astype(jnp.bfloat16)
        d_w_part = jnp.einsum("th,tv->hv", x_full, grad_logits, preferred_element_type=jnp.float32)
        d_w_head = lax.psum_scatter(d_w_part, "fsdp", scatter_dimension=0, tiled=True).astype(jnp.bfloat16)
        return mean_loss.reshape(1), d_hidden, d_w_head

    return jax.shard_map(
        local_step,
        mesh=mesh,
        in_specs=(token_spec, P("fsdp", "tp"), label_spec),
        out_specs=(P("dp"), token_spec, P(("dp", "fsdp"), "tp")),
        check_vma=False,
    )
```

profile of v0, /device:TPU:97, one launch (start us, length us, event | category | flops | bytes accessed | tf_op | source)
XLA Modules:
  0.0 764.7 jit_solution(7031938292791359241)
XLA Ops:
  7.2 0.1 all-gather.4.cloned.1.call-start
  7.2 0.7 all-gather.4.cloned.1.call-update
  8.0 0.1 all-gather.6.cloned.1.call-start
  8.0 0.7 all-gather.6.cloned.1.call-update
  8.8 0.1 reduce-scatter.3.cloned.1.call-start
  8.9 19.7 %all-gather = s32[8,1,512]{2,1,0:T(1,128)S(1)} all-gather(s32[1,1,512]{2,1,0:T(1,128)} %bitcast.25), channel_id=1, replica_groups=mesh['dp'=1,'fsdp'=4,'tp'=8] {'tp'}, dimensions={0}, use_global_device_ids=true | all-gather | bytes 18432 | tf_op jit(solution)/shard_map/all_gather | solution.py:19
  28.6 0.6 broadcast_subtract_fusion
  29.2 31.8 %all-gather.4.cloned.1.call-done = bf16[4096,1024]{1,0:T(8,128)(2,1)} async-done(((bf16[512,1024]{1,0:T(8,128)(2,1)}), bf16[4096,1024]{1,0:T(8,128)(2,1)}) %all-gather.4.cloned.1.call-update) | async-done | bytes 8388624 | tf_op jit(solution)/shard_map/all_gather | solution.py:18
  61.0 122.6 %all-gather.6.cloned.1.call-done = bf16[1024,6288]{0,1:T(8,128)(2,1)} async-done(((bf16[256,6288]{0,1:T(8,128)(2,1)}), bf16[1024,6288]{0,1:T(8,128)(2,1)}) %all-gather.6.cloned.1.call-update) | async-done | bytes 12877840 | tf_op jit(solution)/shard_map/all_gather | solution.py:17
  183.6 0.0 copy-start.4
  183.6 65.0 %fusion.4 = (f32[4096]{0:T(1024)S(1)}, f32[4096,6288]{0,1:T(8,128)}) fusion(bf16[4096,1024]{1,0:T(8,128)(2,1)} %all-gather.4.cloned.1.call-done, bf16[1024,6288]{0,1:T(8,128)(2,1)} %all-gather.6.cloned.1.call-done), kind=kOutput, calls=%fused_computation.12 | convolution fusion | flops 52773318656 | bytes 124305408 | tf_op jit(solution)/shard_map/dot_general | solution.py:20
  248.5 22.7 %pmax.7 = f32[4096]{0:T(1024)S(1)} all-reduce(f32[4096]{0:T(1024)S(1)} %get-tuple-element.7), channel_id=1, replica_groups=mesh['dp'=1,'fsdp'=4,'tp'=8] {'tp'}, use_global_device_ids=true, to_apply=%region_1.0 | all-reduce | flops 4096 | bytes 32768 | tf_op jit(solution)/shard_map/pmax | solution.py:21
  271.2 0.0 copy-start
  271.2 0.0 copy-done.4
  271.2 32.2 %fusion.2 = (f32[4096]{0:T(1024)S(1)}, f32[4096]{0:T(1024)S(1)}) fusion(f32[4096,6288]{0,1:T(8,128)} %get-tuple-element.8, f32[4096]{0:T(1024)S(1)} %pmax.7, s32[4096]{0:T(1024)S(1)} %bitcast.19), kind=kLoop, calls=%fused_computation.6 | loop fusion | flops 128770048 | bytes 103088128 | tf_op jit(solution)/shard_map/reduce_sum | solution.py:25
  303.5 23.9 %psum.14 = f32[2,4096]{1,0:T(2,128)S(1)} all-reduce(f32[2,4096]{1,0:T(2,128)S(1)} %pad_maximum_fusion), channel_id=1, replica_groups=mesh['dp'=1,'fsdp'=4,'tp'=8] {'tp'}, use_global_device_ids=true, to_apply=%region_4.5 | all-reduce | flops 8192 | bytes 65536 | tf_op jit(solution)/shard_map/psum | solution.py:26
  327.3 0.6 fusion.3
  328.0 0.0 copy-start.2
  328.0 0.0 copy-done
  328.0 50.7 %fusion.1 = bf16[4096,6288]{0,1:T(8,128)(2,1)} fusion(f32[4096,6288]{0,1:T(8,128)} %get-tuple-element.8, f32[4096]{0:T(1024)S(1)} %bitcast.17, s32[4096]{0:T(1024)S(1)} %bitcast.20, f32[4096]{0:T(1024)S(1)} %pmax.7), kind=kLoop, calls=%fused_computation.2 | loop fusion | flops 180289536 | bytes 154583040 | tf_op jit(solution)/shard_map/convert_element_type | solution.py:32
  378.6 0.0 copy-done.2
  378.6 63.4 %fusion.5 = f32[4096,1024]{1,0:T(8,128)} fusion(bf16[4096,6288]{0,1:T(8,128)(2,1)} %fusion.1, bf16[1024,6288]{0,1:T(8,128)(2,1)} %all-gather.6.cloned.1.call-done), kind=kOutput, calls=%fused_computation.13 | convolution fusion | flops 52747567104 | bytes 81166336 | tf_op jit(solution)/shard_map/tv,hv->th/dot_general | solution.py:33
  442.1 0.1 reduce-scatter.3.cloned.1.call-update
  442.1 0.0 copy-start.1
  442.1 0.0 copy-start.3
  442.1 0.0 copy-start.5
  442.2 0.3 reduce-scatter.5.cloned.1.call-start
  442.4 62.7 %convolution_bitcast_fusion = f32[1024,6288]{0,1:T(8,128)} fusion(bf16[4096,6288]{0,1:T(8,128)(2,1)} %fusion.1, bf16[4096,1024]{1,0:T(8,128)(2,1)} %all-gather.4.cloned.1.call-done), kind=kOutput, calls=%fused_computation.7 | convolution fusion | flops 52747567104 | bytes 85655552 | tf_op jit(solution)/shard_map/th,tv->hv/dot_general | solution.py:35
  505.1 0.1 reduce-scatter.5.cloned.1.call-update
  505.2 0.0 copy-done.1
  505.2 0.0 copy-done.3
  505.2 0.0 copy-done.5
  505.2 0.6 subtract_reduce_fusion
  505.8 9.2 %psum.15 = f32[]{:T(128)} all-reduce(f32[]{:T(128)} %subtract_reduce_fusion), channel_id=1, replica_groups=mesh['dp'=1,'fsdp'=4,'tp'=8] {'fsdp'}, use_global_device_ids=true, to_apply=%region_6.7 | all-reduce | flops 1 | bytes 8 | tf_op jit(solution)/shard_map/psum | solution.py:30
  515.6 16.1 %reduce-scatter.3.cloned.1.call-done = f32[512,1024]{1,0:T(8,128)} async-done(((f32[4096,1024]{1,0:T(8,128)}), f32[512,1024]{1,0:T(8,128)}) %reduce-scatter.3.cloned.1.call-update) | async-done | bytes 2097168 | tf_op jit(solution)/shard_map/reduce_scatter | solution.py:34
  531.8 2.7 convert_element_type.10
  534.5 217.7 %reduce-scatter.5.cloned.1.call-done = f32[256,6288]{0,1:T(8,128)} async-done(((f32[1024,6288]{0,1:T(8,128)}), f32[256,6288]{0,1:T(8,128)}) %reduce-scatter.5.cloned.1.call-update) | async-done | bytes 6438928 | tf_op jit(solution)/shard_map/reduce_scatter | solution.py:36
  752.2 4.8 convert_element_type.11
  (1 shorter events, 0.0 us)
Async XLA Ops:
  7.2 53.8 %all-gather.4.cloned.1.call-start = ((), (), s32[]{:S(2)}) async-start(), calls=%async_computation.2 | async-start | bytes 9437184 | tf_op jit(solution)/shard_map/all_gather | solution.py:18
  8.0 175.6 %all-gather.6.cloned.1.call-start = ((), (), s32[]{:S(2)}) async-start(), calls=%async_computation.3 | async-start | bytes 16097280 | tf_op jit(solution)/shard_map/all_gather | solution.py:17
  8.8 523.0 %reduce-scatter.3.cloned.1.call-start = ((), (), s32[]{:S(2)}) async-start(), calls=%async_computation.4 | async-start | bytes 18874368 | tf_op jit(solution)/shard_map/reduce_scatter | solution.py:34
  183.6 87.7 %copy-start.4 = (s32[1,8,512]{2,1,0:T(8,128)S(1)}, s32[1,8,512]{2,1,0:T(8,128)}, u32[]{:S(2)}) copy-start(s32[1,8,512]{2,1,0:T(8,128)} %broadcast_subtract_fusion) | copy-start | bytes 49156
  271.2 56.7 %copy-start = (f32[4096]{0:T(1024)}, f32[4096]{0:T(1024)S(1)}, u32[]{:S(2)}) copy-start(f32[4096]{0:T(1024)S(1)} %pmax.7) | copy-start | bytes 49156
  328.0 50.7 %copy-start.2 = (f32[1,4096]{1,0:T(1,128)}, f32[1,4096]{1,0:T(1,128)S(1)}, u32[]{:S(2)}) copy-start(f32[1,4096]{1,0:T(1,128)S(1)} %get-tuple-element.5) | copy-start | bytes 49156
  442.1 63.1 %copy-start.1 = (f32[4096]{0:T(1024)S(1)}, f32[4096]{0:T(1024)}, u32[]{:S(2)}) copy-start(f32[4096]{0:T(1024)} %copy-done) | copy-start | bytes 49156
  442.1 63.1 %copy-start.3 = (f32[1,4096]{1,0:T(1,128)S(1)}, f32[1,4096]{1,0:T(1,128)}, u32[]{:S(2)}) copy-start(f32[1,4096]{1,0:T(1,128)} %copy-done.2) | copy-start | bytes 49156
  442.1 63.1 %copy-start.5 = (f32[1,4096]{1,0:T(1,128)S(1)}, f32[1,4096]{1,0:T(1,128)}, u32[]{:S(2)}) copy-start(f32[1,4096]{1,0:T(1,128)} %get-tuple-element.6) | copy-start | bytes 49156
  442.2 310.0 %reduce-scatter.5.cloned.1.call-start = ((), (), s32[]{:S(2)}) async-start(), calls=%async_computation.5 | async-start | bytes 32194560 | tf_op jit(solution)/shard_map/reduce_scatter | solution.py:36
Sparse Core Ops, SparseCore 0:
  9.6 51.3 all-gather.3
  62.5 120.9 all-gather.5
  442.2 89.4 reduce-scatter.2
  534.0 218.1 reduce-scatter.4
where the time goes:
time: 765 us
  waiting for transfers between devices  390 us (51%)
  matrix products  191 us (25%)
  other arithmetic  91.7 us (12%)
  blocking collectives  75.4 us (10%)
  between operations  15.6 us (2%)
    reduce_scatter x1, waiting for transfers between devices, local_step(): lax.psum_scatter(d_w_part, 'fsdp', scatter_dimension=0, tiled=True)  218 us
    all_gather x1, waiting for transfers between devices, local_step(): w_full = lax.all_gather(w_head, 'fsdp', axis=0, tiled=True)  123 us
    dot_general x1, matrix products, local_step(): logits = jnp.dot(x_full, w_full, preferred_element_type=jnp.float32)  65 us
    dot_general x1, matrix products, local_step(): jnp.einsum('tv,hv->th', grad_logits, w_full, preferred_element_type=jnp.f...  63.4 us
    dot_general x1, matrix products, local_step(): jnp.einsum('th,tv->hv', x_full, grad_logits, preferred_element_type=jnp.f...  62.7 us
    convert_element_type x1, other arithmetic, local_step(): (jnp.where(onehot, prob_rows - 1.0, prob_rows) * inv_tokens).astype(jnp.b...  50.7 us
    reduce_sum x1, other arithmetic, local_step(): jnp.sum(exp_rows, axis=1)  32.2 us
    all_gather x1, waiting for transfers between devices, local_step(): x_full = lax.all_gather(hidden, 'tp', axis=0, tiled=True)  31.8 us
  transfers between devices with their start and end apart: 4, of which 4 were waited for; matrix products, arithmetic and copies ran while one was open for 9% of the time, Pallas kernels for 0%

commit v1 on v0

v1 whole, which is shorter than its diff:
```python
import functools

import jax
import jax.numpy as jnp
from jax import lax
from jax.experimental import pallas as pl
from jax.experimental.pallas import tpu as pltpu
from jax.sharding import PartitionSpec as P

MESH = pl.DeviceIdType.MESH
F32 = jnp.float32
BF16 = jnp.bfloat16
NCH = 5
LOW = -1e30
ANY = pl.BlockSpec(memory_space=pl.ANY)


class Place:
    def __init__(self, nx, ny):
        tp = lax.axis_index("tp")
        self.nx, self.ny = nx, ny
        self.x, self.c, self.y = tp // 2, tp % 2, lax.axis_index("fsdp")
        up, down = (self.y + 1) % ny, (self.y + ny - 1) % ny
        even = (self.y + self.c) % 2 == 0
        self.up, self.down = up, down
        self.p = jnp.where(even, up, down)
        self.a = jnp.where(even, down, up)
        self.far = (self.y + 2) % ny
        self.half = ((self.y - self.c + ny) % ny) // 2

    def dev(self, x=None, y=None, c=None):
        x = self.x if x is None else x
        y = self.y if y is None else y
        c = self.c if c is None else c
        return {"fsdp": y, "tp": x * 2 + c}


def half_of(y, b, ny):
    return ((y - b + ny) % ny) // 2


def remote(src, dst, ssem, rsem, dev):
    return pltpu.make_async_remote_copy(
        src_ref=src, dst_ref=dst, send_sem=ssem, recv_sem=rsem, device_id=dev, device_id_type=MESH
    )


def gather_logits_kernel(
    nx, ny, vocab,
    x_hbm, w_hbm, lab_hbm, xg, wo, z, sta, laba,
    w, xown, ra, rb, xb, zb, bias, m, s, stm,
    xsend, xrecv, ysend, yrecv, wsend, wrecv, dsend, drecv, ssend, srecv, lsend, lrecv, loc, wloc, xsem, zsem,
):
    at = Place(nx, ny)
    x, y, c = at.x, at.y, at.c
    tr = xown.shape[0]
    hk = w_hbm.shape[0]
    sb = w.shape[2] // 2
    slot = NCH * sb
    left, right = (x + nx - 1) % nx, (x + 1) % nx
    far_x = (x + 2) % nx
    top, bot = pl.ds(0, tr // 2), pl.ds(tr // 2, tr // 2)

    barrier = pltpu.get_barrier_semaphore()
    for k in range(1, nx):
        pl.semaphore_signal(barrier, inc=1, device_id=at.dev(x=(x + k) % nx), device_id_type=MESH)
    for k in range(nx):
        pl.semaphore_signal(barrier, inc=1, device_id=at.dev(x=(x + k) % nx, y=at.far), device_id_type=MESH)
    pl.semaphore_signal(barrier, inc=1, device_id=at.dev(y=at.up), device_id_type=MESH)
    pl.semaphore_signal(barrier, inc=1, device_id=at.dev(y=at.down), device_id_type=MESH)
    pl.semaphore_signal(barrier, inc=1, device_id=at.dev(c=1 - c), device_id_type=MESH)
    load_x = pltpu.make_async_copy(x_hbm, xown, loc.at[0])
    load_x.start()
    pl.semaphore_wait(barrier, 2 * nx + 2)
    load_x.wait()

    def x_send(r, to_right):
        i = 0 if to_right else 1
        src = xown if r == 0 else xg.at[1, x]
        return remote(src, xg.at[r, x], xsend.at[r, i], xrecv.at[r, i], at.dev(x=right if to_right else left))

    def x_relay(r, to_right):
        if to_right:
            part = xg.at[r, left, top]
            return remote(part, part, xsend.at[r, 2], xrecv.at[r, 2], at.dev(x=right))
        part = xg.at[r, right, bot]
        return remote(part, part, xsend.at[r, 3], xrecv.at[r, 3], at.dev(x=left))

    y_up = remote(xown.at[top], ra, ysend.at[0], yrecv.at[0], at.dev(y=at.up))
    y_down = remote(xown.at[bot], rb, ysend.at[1], yrecv.at[1], at.dev(y=at.down))
    y_up2 = remote(ra, xg.at[1, x, top], ysend.at[2], yrecv.at[2], at.dev(y=at.up))
    y_down2 = remote(rb, xg.at[1, x, bot], ysend.at[3], yrecv.at[3], at.dev(y=at.down))
    keep_x = pltpu.make_async_copy(xown, xg.at[0, x], loc.at[1])

    def w_src(f, q):
        return w_hbm.at[:, pl.ds(pl.multiple_of(f * slot + q * sb, 128), sb)]

    def w_dst(k, q):
        return w.at[q, pl.ds(pl.multiple_of(k * hk, 16), hk), pl.ds(pl.multiple_of(c * sb, 128), sb)]

    def w_own(q):
        return remote(w_src(at.half, q), w_dst(y, q), wsend.at[0, q], wrecv.at[0, q], at.dev(y=at.p))

    def w_other(q):
        return remote(w_src(1 - at.half, q), w_dst(y, q), wsend.at[1, q], wrecv.at[1, q], at.dev(y=at.a))

    def w_fwd(q):
        return remote(w_dst(at.a, q), w_dst(at.a, q), wsend.at[2, q], wrecv.at[2, q], at.dev(y=at.p))

    def w_core(q):
        part = w.at[q, :, pl.ds(pl.multiple_of(c * sb, 128), sb)]
        return remote(part, part, dsend.at[q], drecv.at[q], at.dev(c=1 - c))

    def w_local(q):
        return pltpu.make_async_copy(w_src(at.half, q), w_dst(y, q), wloc.at[q])

    y_up.start()
    y_down.start()
    x_send(0, True).start()
    x_send(0, False).start()
    w_own(0).start()
    w_other(0).start()
    keep_x.start()
    for q in range(NCH):
        w_local(q).start()

    peers = [(0, k) for k in range(1, nx)] + [(1, k) for k in range(nx)]

    def lab_copy(i):
        sy, k = peers[i]
        return remote(
            lab_hbm, laba.at[sy, x], lsend.at[i], lrecv.at[sy, x],
            at.dev(x=(x + k) % nx, y=at.far if sy else y),
        )

    for i in range(len(peers)):
        lab_copy(i).start()
    lab_own = pltpu.make_async_copy(lab_hbm, laba.at[0, x], loc.at[2])
    lab_own.start()

    col = lax.broadcasted_iota(jnp.int32, bias.shape, 1)
    row = lax.broadcasted_iota(jnp.int32, bias.shape, 0)
    b = col // sb
    pos = row * sb + col - b * sb
    half_b = jnp.where(b == 0, half_of(y, 0, ny), half_of(y, 1, ny))
    bias[...] = jnp.where((half_b == 1) & (pos >= vocab - slot), LOW, 0.0)
    m[...] = jnp.full_like(m, -3e38)
    s[...] = jnp.zeros_like(s)

    y_up.wait_recv()
    y_up2.start()
    y_down.wait_recv()
    y_down2.start()
    for q in range(1, NCH):
        w_own(q).start()
        w_other(q).start()
    w_other(0).wait_recv()
    w_fwd(0).start()
    x_send(0, True).wait_recv()
    x_relay(0, True).start()
    x_send(0, False).wait_recv()
    x_relay(0, False).start()
    y_up2.wait_recv()
    y_down2.wait_recv()
    x_send(1, True).start()
    x_send(1, False).start()
    keep_x.wait()
    x_relay(0, True).wait_recv()
    x_relay(0, False).wait_recv()

    n_steps = 2 * nx * NCH

    def place_of(i):
        g = i // nx
        r = g // NCH
        k = i - g * nx
        return r, g - r * NCH, k

    def xcp(i, u):
        r, j, k = place_of(i)
        return pltpu.make_async_copy(xg.at[r, k], xb.at[u], xsem.at[u])

    def zcp(i, u):
        r, j, k = place_of(i)
        return pltpu.make_async_copy(zb.at[u], z.at[j, r, k], zsem.at[u])

    def step(i, u):
        r, j, k = place_of(i)
        run = r * nx + k
        c0 = 0
        for width in (sb * 4 // 5, 2 * sb - sb * 4 // 5) if sb % 640 == 0 else (2 * sb,):
            cols = slice(c0, c0 + width)
            zz = jnp.dot(xb[u], w[j, :, cols], preferred_element_type=F32) + bias[pl.ds(j, 1), cols]
            zb[u, :, cols] = zz
            blk = min(64, tr)
            for o in range(0, tr, blk):
                rows = slice(o, o + blk)
                m_old = m[run, rows, :]
                parts = [zz[rows, 128 * e : 128 * e + 128] for e in range(width // 128)]
                mx = m_old
                for part in parts:
                    mx = jnp.maximum(mx, part)
                acc = s[run, rows, :] * jnp.exp(m_old - mx)
                for part in parts:
                    acc = acc + jnp.exp(part - mx)
                m[run, rows, :] = mx
                s[run, rows, :] = acc
            c0 += width

    def stat_copy(r, i):
        sy, k = peers[i]
        rr = 1 - r if sy else r
        return remote(
            stm.at[r], sta.at[sy, x, rr], ssend.at[r, i], srecv.at[sy, x, rr],
            at.dev(x=(x + k) % nx, y=at.far if sy else y),
        )

    def stat_own(r):
        return pltpu.make_async_copy(stm.at[r], sta.at[0, x, r], loc.at[3 + r])

    def finish_stats(r):
        def one(d, _):
            run = r * nx + d
            mm = m[run]
            top_m = jnp.max(mm, axis=1, keepdims=True)
            tot = jnp.sum(s[run] * jnp.exp(mm - top_m), axis=1, keepdims=True)
            lane = lax.broadcasted_iota(jnp.int32, mm.shape, 1)
            blk = jnp.where(lane == 0, top_m, jnp.where(lane == 1, tot, 0.0))
            stm[r, d] = blk.T[0:8, :]
            return 0

        lax.fori_loop(0, nx, one, 0)
        for i in range(len(peers)):
            stat_copy(r, i).start()
        stat_own(r).start()

    def body(t, _):
        @pl.when((t < 2 * NCH) & (t % 2 == 0))
        def _():
            j = t // 2
            w_local(j).wait()
            w_own(j).wait_recv()
            w_fwd(j).wait_recv()
            w_core(j).start()

            @pl.when(j + 1 < NCH)
            def _():
                w_other(j + 1).wait_recv()
                w_fwd(j + 1).start()

            w_core(j).wait_recv()

        @pl.when(t == 6)
        def _():
            x_send(1, True).wait_recv()
            x_relay(1, True).start()
            x_send(1, False).wait_recv()
            x_relay(1, False).start()

        @pl.when(t == 2 * NCH - 1)
        def _():
            pltpu.make_async_copy(w, wo, loc.at[5]).start()
            x_relay(1, True).wait_recv()
            x_relay(1, False).wait_recv()

        @pl.when(t == 2 * NCH)
        def _():
            finish_stats(0)

        for u in range(2):
            xcp(2 * t + u, u).wait()

        @pl.when(t > 0)
        def _():
            for u in range(2):
                zcp(2 * t - 2 + u, u).wait()

        for u in range(2):
            step(2 * t + u, u)
        for u in range(2):
            zcp(2 * t + u, u).start()

        @pl.when(2 * t + 2 < n_steps)
        def _():
            for u in range(2):
                xcp(2 * t + 2 + u, u).start()

        return 0

    for u in range(2):
        xcp(u, u).start()
    lax.fori_loop(0, n_steps // 2, body, 0)
    finish_stats(1)
    for u in range(2):
        zcp(n_steps - 2 + u, u).wait()
    pltpu.make_async_copy(w, wo, loc.at[5]).wait()
    lab_own.wait()
    stat_own(0).wait()
    stat_own(1).wait()
    for r in range(2):
        for right_way in (True, False):
            x_send(r, right_way).wait_send()
            x_relay(r, right_way).wait_send()
    for cp in (y_up, y_down, y_up2, y_down2):
        cp.wait_send()
    for q in range(NCH):
        w_own(q).wait_send()
        w_other(q).wait_send()
        w_fwd(q).wait_send()
        w_core(q).wait_send()
    for i in range(len(peers)):
        lab_copy(i).wait_send()
        stat_copy(0, i).wait_send()
        stat_copy(1, i).wait_send()
    for sy in range(2):
        for k in range(nx):
            def arrived():
                remote(lab_hbm, laba.at[sy, k], lsend.at[0], lrecv.at[sy, k], at.dev(c=1 - c)).wait_recv()
                for rr in range(2):
                    remote(stm.at[rr], sta.at[sy, k, rr], ssend.at[0, 0], srecv.at[sy, k, rr], at.dev(c=1 - c)).wait_recv()

            if sy == 0:
                pl.when(k != x)(arrived)
            else:
                arrived()


def gather_logits(nx, ny, vocab, x, w, lab):
    tr, h = x.shape
    hk, vp = w.shape
    ch = vp // NCH
    shape = jax.ShapeDtypeStruct
    dma = pltpu.SemaphoreType.DMA
    vm = pltpu.VMEM
    flops = 2 * 2 * nx * tr * h * vp
    return pl.pallas_call(
        functools.partial(gather_logits_kernel, nx, ny, vocab),
        out_shape=(
            shape((2, nx, tr, h), BF16),
            shape((NCH, h, ch), BF16),
            shape((NCH, 2, nx, tr, ch), F32),
            shape((2, nx, 2, nx, 8, tr), F32),
            shape((2, nx) + lab.shape, jnp.int32),
        ),
        in_specs=[ANY] * 3,
        out_specs=(ANY,) * 5,
        scratch_shapes=[
            vm((NCH, h, ch), BF16), vm((tr, h), BF16), vm((tr // 2, h), BF16), vm((tr // 2, h), BF16),
            vm((2, tr, h), BF16), vm((2, tr, ch), F32), vm((8, ch), F32),
            vm((2 * nx, tr, 128), F32), vm((2 * nx, tr, 128), F32), vm((2, nx, 8, tr), F32),
            dma((2, 4)), dma((2, 4)), dma((4,)), dma((4,)), dma((3, NCH)), dma((3, NCH)), dma((NCH,)), dma((NCH,)),
            dma((2, 2 * nx - 1)), dma((2, nx, 2)), dma((2 * nx - 1,)), dma((2, nx)),
            dma((6,)), dma((NCH,)), dma((2,)), dma((2,)),
        ],
        compiler_params=pltpu.CompilerParams(
            collective_id=0, has_side_effects=True, vmem_limit_bytes=60 * 2**20
        ),
        cost_estimate=pl.CostEstimate(flops=flops, bytes_accessed=4 * 2 * nx * tr * vp, transcendentals=0),
        name="gather_logits",
    )(x, w, lab)


def grads_kernel(nx, inv, z, w_hbm, xg, st8, dxp, dwp, loss, w, xt, zb, gb, acc, dx, st, lacc, zsem, sem, osem):
    tr, h = xg.shape[2], xg.shape[3]
    ch = zb.shape[2]
    pltpu.make_async_copy(w_hbm, w, sem.at[0]).start()

    def prep(run, _):
        cp = pltpu.make_async_copy(xg.at[run // nx, run % nx], gb.at[:, pl.ds(0, h)], sem.at[1])
        cp.start()
        one = st8[run // nx, run % nx]
        st[run] = jnp.concatenate([one] * 16, axis=0).T
        cp.wait()
        xt[run] = gb[:, 0:h].T
        return 0

    lax.fori_loop(0, 2 * nx, prep, 0)
    lacc[...] = jnp.zeros_like(lacc)
    pltpu.make_async_copy(w_hbm, w, sem.at[0]).wait()
    n_each = 2 * nx * NCH

    def place_of(i):
        first = i < n_each
        k = jnp.where(first, i, i - n_each)
        j = jnp.where(first, k % NCH, k // (2 * nx))
        run = jnp.where(first, k // NCH, k % (2 * nx))
        return j, run

    def zcp(i, u):
        j, run = place_of(i)
        return pltpu.make_async_copy(z.at[j, run // nx, run % nx], zb.at[u], zsem.at[u])

    def make_g(i, u, want_loss):
        j, run = place_of(i)
        blk = min(64, tr)
        for o in range(0, tr, blk):
            rows = slice(o, o + blk)
            t = st[run, rows, :]
            top = jnp.broadcast_to(t[:, 0:1], (blk, 128))
            scale = jnp.broadcast_to(t[:, 1:2], (blk, 128))
            lab = jnp.broadcast_to(t[:, 2:3], (blk, 128)).astype(jnp.int32) - j * ch
            lane = lax.broadcasted_iota(jnp.int32, (blk, 128), 1)
            add = jnp.zeros((blk, 128), F32)
            for e in range(ch // 128):
                cols = slice(128 * e, 128 * e + 128)
                d = zb[u, rows, cols] - top
                g = jnp.exp(d) * scale
                hit = lab - 128 * e == lane
                if want_loss:
                    add = add + jnp.where(hit, d, 0.0)
                gb[rows, cols] = jnp.where(hit, g - inv, g).astype(BF16)
            if want_loss:
                lacc[rows, :] += add

    def dx_body(t, _):
        for u in range(2):
            i = 2 * t + u
            zcp(i, u).wait()
            zcp(i + 1, 1 - u).start()
            j, run = place_of(i)
            make_g(i, u, True)
            part = lax.dot_general(gb[...], w[j], (((1,), (1,)), ((), ())), preferred_element_type=F32)

            @pl.when(j == 0)
            def _():
                dx[...] = part

            @pl.when(j > 0)
            def _():
                dx[...] += part

            @pl.when(j == NCH - 1)
            def _():
                cp = pltpu.make_async_copy(dx, dxp.at[run // nx, run % nx], osem.at[0])
                cp.start()
                cp.wait()

        return 0

    def dw_body(t, _):
        for u in range(2):
            i = n_each + 2 * t + u
            zcp(i, u).wait()

            @pl.when(i + 1 < 2 * n_each)
            def _():
                zcp(i + 1, 1 - u).start()

            j, run = place_of(i)
            make_g(i, u, False)
            part = jnp.dot(xt[run], gb[...], preferred_element_type=F32)

            @pl.when(run == 0)
            def _():
                acc[...] = part

            @pl.when(run > 0)
            def _():
                acc[...] += part

            @pl.when(run == 2 * nx - 1)
            def _():
                cp = pltpu.make_async_copy(acc, dwp.at[j], osem.at[0])
                cp.start()
                cp.wait()

        return 0

    zcp(0, 0).start()
    lax.fori_loop(0, n_each // 2, dx_body, 0)
    lax.fori_loop(0, n_each // 2, dw_body, 0)
    loss[...] = jnp.sum(lacc[...].reshape(tr // 8, 8, 128), axis=0)


def grads(nx, inv, z, w, xg, st8):
    tr, h = xg.shape[2:]
    ch = w.shape[2]
    shape = jax.ShapeDtypeStruct
    dma = pltpu.SemaphoreType.DMA
    vm = pltpu.VMEM
    vspec = pl.BlockSpec(memory_space=pltpu.VMEM)
    return pl.pallas_call(
        functools.partial(grads_kernel, nx, inv),
        out_shape=(shape((2, nx, tr, h), F32), shape((NCH, h, ch), F32), shape((8, 128), F32)),
        in_specs=[ANY, ANY, ANY, vspec],
        out_specs=(ANY, ANY, vspec),
        scratch_shapes=[
            vm((NCH, h, ch), BF16), vm((2 * nx, h, tr), BF16), vm((2, tr, ch), F32), vm((tr, ch), BF16),
            vm((h, ch), F32), vm((tr, h), F32), vm((2 * nx, tr, 128), F32), vm((tr, 128), F32),
            dma((2,)), dma((2,)), dma((1,)),
        ],
        compiler_params=pltpu.CompilerParams(vmem_limit_bytes=63 * 2**20),
        name="grads",
    )(z, w, xg, st8)


def solution(mesh):
    ny = mesh.shape["fsdp"]
    tp_size = mesh.shape["tp"]
    nx = tp_size // 2
    token_spec = P(("dp", "fsdp", "tp"), None)
    label_spec = P(("dp", "fsdp", "tp"))

    def local_step(hidden, w_head, labels):
        tr, h = hidden.shape
        hk, vocab = w_head.shape
        inv = 1.0 / (tr * tp_size * ny)
        vp = -(-vocab // (256 * NCH)) * (256 * NCH)
        ch = vp // NCH
        sb = ch // 2
        slot = NCH * sb
        tp = lax.axis_index("tp")
        x, c, y = tp // 2, tp % 2, lax.axis_index("fsdp")
        w_pad = jnp.pad(w_head, ((0, 0), (0, vp - vocab)))
        lab8 = jnp.pad(labels.reshape(-1, 128), ((0, 8 - tr // 128), (0, 0)))
        xg, wg, z, sta, laba = gather_logits(nx, ny, vocab, hidden, w_pad, lab8)

        ms = sta[..., 0, :].reshape(2 * nx, 2, nx, tr)
        ss = sta[..., 1, :].reshape(2 * nx, 2, nx, tr)
        top = jnp.max(ms, axis=0)
        tot = jnp.sum(ss * jnp.exp(ms - top), axis=0)
        lab = laba[:, :, 0 : tr // 128, :].reshape(2, nx, tr)
        shard, off = lab // vocab, lab % vocab
        b, f = shard % 2, off // slot
        pos = off - f * slot
        mine = (shard // 2 == x) & (half_of(y, b, ny) == f)
        col = jnp.where(mine, (pos // sb) * ch + b * sb + pos % sb, -1)
        rows = [top, inv / tot, col.astype(F32)]
        st8 = jnp.stack(rows + [jnp.zeros_like(top)] * 5, axis=2)
        dxp, dwp, lpart = grads(nx, inv, z, wg, xg, st8)

        log_own = jnp.sum(jnp.log(lax.dynamic_index_in_dim(tot[0], x, keepdims=False)))
        mean_loss = lax.psum(log_own - jnp.sum(lpart), ("fsdp", "tp")) * inv

        groups = [[2 * k + e for k in range(nx)] for e in range(2)]
        own = lax.psum_scatter(dxp[0], "tp", scatter_dimension=0, tiled=False, axis_index_groups=groups)
        oth = lax.psum_scatter(dxp[1], "tp", scatter_dimension=0, tiled=False, axis_index_groups=groups)
        oth = lax.ppermute(oth, "fsdp", [(k, (k + 2) % ny) for k in range(ny)])
        d_hidden = (own + oth).astype(BF16)

        dw = jnp.transpose(dwp.reshape(NCH, h, 2, sb), (2, 1, 0, 3)).reshape(2, h, slot)
        dw = dw + lax.ppermute(dw, "tp", [(k, k ^ 1) for k in range(tp_size)])
        mesh_axes = ("fsdp", "tp")

        def par(yy, bb):
            return (yy + 1) % ny if (yy + bb) % 2 == 0 else (yy - 1) % ny

        def adj(yy, bb):
            return (yy - 1) % ny if (yy + bb) % 2 == 0 else (yy + 1) % ny

        outs = []
        for bb in range(2):
            perm = [(yy * tp_size + t, par(yy, bb) * tp_size + t) for yy in range(ny) for t in range(tp_size)]
            outs.append(dw[bb] + lax.ppermute(dw[bb], mesh_axes, perm))
        mine_dw = jnp.where(c == 0, outs[0], outs[1])
        adj_perm = [
            (yy * tp_size + t, adj(yy, t % 2) * tp_size + t) for yy in range(ny) for t in range(tp_size)
        ]
        even = (y + c) % 2 == 0
        adj_row = jnp.where(even, (y + ny - 1) % ny, (y + 1) % ny)
        keep = lax.dynamic_slice_in_dim(mine_dw, y * hk, hk, axis=0)
        give = lax.dynamic_slice_in_dim(mine_dw, adj_row * hk, hk, axis=0)
        got = lax.ppermute(give, mesh_axes, adj_perm)
        hh = half_of(y, c, ny)
        first = jnp.where(hh == 0, keep, got)
        second = jnp.where(hh == 0, got, keep)
        d_w = jnp.concatenate([first, second], axis=1)[:, :vocab].astype(BF16)
        return mean_loss.reshape(1), d_hidden, d_w

    return jax.shard_map(
        local_step,
        mesh=mesh,
        in_specs=(token_spec, P("fsdp", "tp"), label_spec),
        out_specs=(P("dp"), token_spec, P(("dp", "fsdp"), "tp")),
        check_vma=False,
    )
```

time: 765 us -> 1030 us (1.35)
  Pallas kernels: 0 us -> 450 us
  matrix products: 191 us -> 0 us
  local copies, waits for them, and re-layouts: 0.66 us -> 113 us
  waiting for transfers between devices: 390 us -> 307 us
  other arithmetic: 91.7 us -> 57.5 us
    pallas_call x0 -> x2, Pallas kernels: none -> 450 us  [the longest x1 250 us: grads(): pl.pallas_call(functools.partial(grads_kernel, nx, inv), out_shape=(shape...]
    ppermute x0 -> x5, waiting for transfers between devices: none -> 305 us  [the longest x2 277 us: local_step(): outs.append(dw[bb] + lax.ppermute(dw[bb], mesh_axes, perm))]
    reduce_scatter x2, waiting for transfers between devices: 234 us -> 2.48 us  [the longest x1 2.46 us: local_step(): lax.psum_scatter(dxp[1], 'tp', scatter_dimension=0, tiled=False, axis_ind...]
    dot_general x3 -> x0, matrix products: 191 us -> none  [the longest x1 65 us: local_step(): logits = jnp.dot(x_full, w_full, preferred_element_type=jnp.float32)]
    all_gather x2 -> x0, waiting for transfers between devices: 154 us -> none  [the longest x1 123 us: local_step(): w_full = lax.all_gather(w_head, 'fsdp', axis=0, tiled=True)]
    convert_element_type x3 -> x2, other arithmetic: 58.2 us -> 3.41 us  [the longest x1 2.86 us: local_step(): d_hidden = (own + oth).astype(BF16)]
    psum x2 -> x1, blocking collectives: 33 us -> 78.4 us  [local_step(): mean_loss = lax.psum(log_own - jnp.sum(lpart), ('fsdp', 'tp')) * inv]
    transpose x0 -> x1, local copies, waits for them, and re-layouts: none -> 38.3 us  [local_step(): jnp.transpose(dwp.reshape(NCH, h, 2, sb), (2, 1, 0, 3)).reshape(2, h, slot)]
  transfers between devices with their start and end apart: 4 -> 7, of which waited for: 4 -> 4; matrix products, arithmetic and copies ran while one was open for 9% -> 8% of each run, Pallas kernels for 0% -> 0%
where the time goes in v1:
time: 1030 us
  Pallas kernels  450 us (44%)
  waiting for transfers between devices  307 us (30%)
  local copies, waits for them, and re-layouts  113 us (11%)
  blocking collectives  78.4 us (8%)
  other arithmetic  57.5 us (6%)
  between operations  17.4 us (2%)
    ppermute x2, waiting for transfers between devices, local_step(): outs.append(dw[bb] + lax.ppermute(dw[bb], mesh_axes, perm))  277 us
    pallas_call x1, Pallas kernels, grads(): pl.pallas_call(functools.partial(grads_kernel, nx, inv), out_shape=(shape...  250 us
    pallas_call x1, Pallas kernels, gather_logits(): pl.pallas_call(functools.partial(gather_logits_kernel, nx, ny, vocab), ou...  200 us
    psum x1, blocking collectives, local_step(): mean_loss = lax.psum(log_own - jnp.sum(lpart), ('fsdp', 'tp')) * inv  78.4 us
    transpose x1, local copies, waits for them, and re-layouts, local_step(): jnp.transpose(dwp.reshape(NCH, h, 2, sb), (2, 1, 0, 3)).reshape(2, h, slot)  38.3 us
    reshape x1, local copies, waits for them, and re-layouts, local_step(): dwp.reshape(NCH, h, 2, sb)  31.8 us
    ppermute x1, waiting for transfers between devices, local_step(): dw = dw + lax.ppermute(dw, 'tp', [(k, k ^ 1) for k in range(tp_size)])  27.2 us
    add x1, other arithmetic, local_step(): dw = dw + lax.ppermute(dw, 'tp', [(k, k ^ 1) for k in range(tp_size)])  26 us
  transfers between devices with their start and end apart: 7, of which 4 were waited for; matrix products, arithmetic and copies ran while one was open for 8% of the time, Pallas kernels for 0%

profile of v1, /device:TPU:97, one launch (start us, length us, event | category | flops | bytes accessed | tf_op | source)
XLA Modules:
  0.0 1031.1 jit_solution(13445399105428836098)
XLA Ops:
  7.2 0.1 reduce-scatter.5.cloned.1.call-start
  7.3 4.0 copy.8
  11.3 1.3 pad.9.lab_hbm
  12.6 1.9 pad.8.w_hbm
  14.4 200.2 %gather_logits.1 = (bf16[2,4,512,1024]{3,2,1,0:T(8,128)(2,1)}, bf16[5,1024,1280]{2,1,0:T(8,128)(2,1)}, f32[5,2,4,512,1280]{4,3,2,1,0:T(8,128)}, f32[2,4,2,4,8,512]{5,4,3,2,1,0:T(8,128)}, s32[2,4,8,128]{3,2,1,0:T(8,128)}) custom-call(bf16[512,1024]{1,0:T(8,128)(2,1)} %x_hbm.1, bf16[256,6400]{1,0:T(8,128)(2,1)} %pad.8.w_hbm, s32[8,128]{1,0:T(8,128)} %pad.9.lab_hbm), custom_call_target="tpu_custom_call" | custom-call | flops 53687091200 | bytes 104857600 | tf_op jit(solution)/shard_map/gather_logits/pallas_call | solution.py:336
  214.6 1.4 slice_reduce_fusion
  216.0 2.0 multiply_reduce_fusion
  218.0 0.8 slice_divide_fusion
  218.8 0.8 sign_compare_fusion
  219.6 0.6 fusion.3
  220.2 0.8 stack.13.st8
  221.0 250.1 %grads.1 = (f32[2,4,512,1024]{3,2,1,0:T(8,128)}, f32[5,1024,1280]{2,1,0:T(8,128)}, f32[8,128]{1,0:T(8,128)}) custom-call(f32[5,2,4,512,1280]{4,3,2,1,0:T(8,128)} %get-tuple-element.12.z, bf16[5,1024,1280]{2,1,0:T(8,128)(2,1)} %get-tuple-element.13.w_hbm, bf16[2,4,512,1024]{3,2,1,0:T(8,128)(2,1)} %get-tuple-element.14.xg, f32[2,4,8,512]{3,2,1,0:T(8,128)} %stack.13.st8), custom_call_target="tpu_custom_call" | custom-call | tf_op jit(solution)/shard_map/grads/pallas_call | solution.py:482
  471.1 31.8 %reshape.337 = f32[5,1024,2,640]{3,2,1,0:T(2,128)} reshape(f32[5,1024,1280]{2,1,0:T(8,128)} %get-tuple-element.18) | data formatting | bytes 52428800 | tf_op jit(solution)/shard_map/reshape | solution.py:541
  502.9 38.3 %copy.10 = f32[2,1024,5,640]{1,3,2,0:T(8,128)} copy(f32[2,1024,5,640]{3,0,1,2:T(2,128)} %bitcast.25) | data formatting | bytes 52428800 | tf_op jit(solution)/shard_map/transpose | solution.py:541
  541.2 2.2 collective-permute-start.1
  543.4 11.0 %slice_bitcast_fusion.3 = (f32[4,512,1024]{2,1,0:T(8,128)}, f32[4,512,1024]{2,1,0:T(8,128)}) fusion(f32[2,4,512,1024]{3,2,1,0:T(8,128)} %get-tuple-element.17), kind=kLoop, calls=%fused_computation.4 | loop fusion | bytes 33554432 | tf_op jit(solution)/shard_map/squeeze | solution.py:536
  554.4 0.1 reduce-scatter.5.cloned.1.call-update
  554.5 0.1 reduce-scatter.3.cloned.1.call-start
  554.6 27.2 %collective-permute-done.1 = f32[2,1024,3200]{1,2,0:T(8,128)} collective-permute-done((f32[2,1024,3200]{1,2,0:T(8,128)}, f32[2,1024,3200]{1,2,0:T(8,128)}, u32[]{:S(2)}, u32[]{:S(2)}) %collective-permute-start.1) | collective-permute-done | bytes 26214432 | tf_op jit(solution)/shard_map/ppermute | solution.py:542
  581.7 26.0 %bitcast_add_fusion.1 = f32[2,1024,3200]{1,2,0:T(8,128)} fusion(f32[2,1024,3200]{1,2,0:T(8,128)} %collective-permute-done.1, f32[2,1024,5,640]{1,3,2,0:T(8,128)} %copy.10), kind=kLoop, calls=%fused_computation.39 | loop fusion | flops 6553600 | bytes 78643200 | tf_op jit(solution)/shard_map/add | solution.py:542
  607.7 20.1 %slice_bitcast_fusion.1 = (f32[1024,3200]{0,1:T(8,128)}, f32[1024,3200]{0,1:T(8,128)}) fusion(f32[2,1024,3200]{1,2,0:T(8,128)} %bitcast_add_fusion.1), kind=kLoop, calls=%fused_computation.1 | loop fusion | bytes 52428800 | tf_op jit(solution)/shard_map/squeeze | solution.py:554
  627.9 1.8 collective-permute-start.3
  629.7 0.0 collective-permute-start.2
  629.7 0.1 reduce-scatter.3.cloned.1.call-update
  629.8 2.5 reduce-scatter.5.cloned.1.call-done
  632.2 0.0 copy-start.1
  632.3 2.8 collective-permute-start
  635.0 277.0 %collective-permute-done.3 = f32[1024,3200]{0,1:T(8,128)} collective-permute-done((f32[1024,3200]{0,1:T(8,128)}, f32[1024,3200]{0,1:T(8,128)}, u32[]{:S(2)}, u32[]{:S(2)}) %collective-permute-start.3) | collective-permute-done | bytes 13107232 | tf_op jit(solution)/shard_map/ppermute | solution.py:554
  912.0 0.4 collective-permute-done.2
  912.3 17.5 %add_select_fusion = bf16[1024,3200]{0,1:T(8,128)(2,1)S(1)} fusion(f32[1024,3200]{0,1:T(8,128)} %collective-permute-done.3, f32[1024,3200]{0,1:T(8,128)} %collective-permute-done.2, pred[]{:T(512)S(6)} %eq.48, f32[2,1024,3200]{1,2,0:T(8,128)} %bitcast_add_fusion.1), kind=kLoop, calls=%fused_computation.2 | loop fusion | flops 9830400 | bytes 58982400 | tf_op jit(solution)/shard_map/jit(_where)/select_n | solution.py:555
  929.9 0.0 copy-start
  929.9 2.7 copy-done
  932.6 1.4 constant_dynamic-slice_fusion
  934.0 0.3 collective-permute-start.4
  934.3 0.0 copy-done.1
  934.3 0.6 reduce_sum.29
  934.9 0.6 log_reduce_fusion
  936.8 78.4 %psum.7 = f32[]{:T(128)} all-reduce(f32[]{:T(128)S(6)} %sub.81), channel_id=1, replica_groups=mesh['dp'=1,'fsdp'=4,'tp'=8] {'fsdp','tp'}, use_global_device_ids=true, to_apply=%region_4.5 | all-reduce | flops 1 | bytes 8 | tf_op jit(solution)/shard_map/psum | solution.py:533
  1015.8 0.0 reduce-scatter.3.cloned.1.call-done
  1015.8 0.0 collective-permute-done
  1015.8 2.9 fusion
  1018.7 0.0 collective-permute-done.4
  1018.7 2.6 select_convert_fusion.1
  1021.2 1.9 pad_maximum_fusion
  (7 shorter events, 0.1 us)
Async XLA Ops:
  7.2 625.1 %reduce-scatter.5.cloned.1.call-start = ((), (), s32[]{:S(2)}) async-start(), calls=%async_computation.3 | async-start | bytes 10485760 | tf_op jit(solution)/shard_map/reduce_scatter | solution.py:537
  541.2 40.5 %collective-permute-start.1 = (f32[2,1024,3200]{1,2,0:T(8,128)}, f32[2,1024,3200]{1,2,0:T(8,128)}, u32[]{:S(2)}, u32[]{:S(2)}) collective-permute-start(f32[2,1024,3200]{1,2,0:T(8,128)} %bitcast.24), channel_id=1, source_target_pairs={{0,1},{1,0},{2,3},{3,2},{4,5},{5,4},{6,7},{7,6},{8,9},{9,8},{10,11... | collective-permute-start | bytes 78643208 | tf_op jit(solution)/shard_map/ppermute | solution.py:542
  554.5 461.3 %reduce-scatter.3.cloned.1.call-start = ((), (), s32[]{:S(2)}) async-start(), calls=%async_computation.2 | async-start | bytes 10485760 | tf_op jit(solution)/shard_map/reduce_scatter | solution.py:536
  627.9 284.1 %collective-permute-start.3 = (f32[1024,3200]{0,1:T(8,128)}, f32[1024,3200]{0,1:T(8,128)}, u32[]{:S(2)}, u32[]{:S(2)}) collective-permute-start(f32[1024,3200]{0,1:T(8,128)} %get-tuple-element.20), channel_id=1, source_target_pairs={{0,24},{1,25},{2,26},{3,27},{4,28},{5,29},{6,30},{7,31},{8,16},{9,... | collective-permute-start | bytes 39321608 | tf_op jit(solution)/shard_map/ppermute | solution.py:554
  629.7 282.7 %collective-permute-start.2 = (f32[1024,3200]{0,1:T(8,128)}, f32[1024,3200]{0,1:T(8,128)}, u32[]{:S(2)}, u32[]{:S(2)}) collective-permute-start(f32[1024,3200]{0,1:T(8,128)} %get-tuple-element.19), channel_id=1, source_target_pairs={{0,8},{1,9},{2,10},{3,11},{4,12},{5,13},{6,14},{7,15},{8,0},{9,1},... | collective-permute-start | bytes 39321608 | tf_op jit(solution)/shard_map/ppermute | solution.py:554
  632.2 302.0 %copy-start.1 = (f32[8,128]{1,0:T(8,128)S(1)}, f32[8,128]{1,0:T(8,128)}, u32[]{:S(2)}) copy-start(f32[8,128]{1,0:T(8,128)} %get-tuple-element.16) | copy-start | bytes 12292
  632.3 383.6 %collective-permute-start = (f32[512,1024]{1,0:T(8,128)}, f32[512,1024]{1,0:T(8,128)S(1)}, u32[]{:S(2)}, u32[]{:S(2)}) collective-permute-start(f32[512,1024]{1,0:T(8,128)} %bitcast.29), channel_id=1, source_target_pairs={{0,16},{8,24},{16,0},{24,8},{1,17},{9,25},{17,1},{25,9},{2,18},{10... | collective-permute-start | bytes 6291464 | tf_op jit(solution)/shard_map/ppermute | solution.py:538
  929.9 2.7 copy-start
  934.0 84.7 %collective-permute-start.4 = (bf16[256,3200]{0,1:T(8,128)(2,1)}, bf16[256,3200]{0,1:T(8,128)(2,1)}, u32[]{:S(2)}, u32[]{:S(2)}) collective-permute-start(bf16[256,3200]{0,1:T(8,128)(2,1)} %constant_dynamic-slice_fusion), channel_id=1, source_target_pairs={{0,24},{1,9},{2,26},{3,11},{4,28},{5,13},{6,30},{7,15},{8,16},{9,1... | collective-permute-start | bytes 4915208 | tf_op jit(solution)/shard_map/ppermute | solution.py:563
Sparse Core Ops, SparseCore 0:
  554.6 77.5 reduce-scatter.4
  634.6 77.6 reduce-scatter.2

commit v2 on v1

v2 whole, which is shorter than its diff:
```python
import functools

import jax
import jax.numpy as jnp
from jax import lax
from jax.experimental import pallas as pl
from jax.experimental.pallas import tpu as pltpu
from jax.sharding import PartitionSpec as P

MESH = pl.DeviceIdType.MESH
F32 = jnp.float32
BF16 = jnp.bfloat16
NCH = 5
LOW = -1e30
ANY = pl.BlockSpec(memory_space=pl.ANY)


class Place:
    def __init__(self, nx, ny):
        tp = lax.axis_index("tp")
        self.nx, self.ny = nx, ny
        self.x, self.c, self.y = tp // 2, tp % 2, lax.axis_index("fsdp")
        up, down = (self.y + 1) % ny, (self.y + ny - 1) % ny
        even = (self.y + self.c) % 2 == 0
        self.up, self.down = up, down
        self.p = jnp.where(even, up, down)
        self.a = jnp.where(even, down, up)
        self.far = (self.y + 2) % ny
        self.half = ((self.y - self.c + ny) % ny) // 2

    def dev(self, x=None, y=None, c=None):
        x = self.x if x is None else x
        y = self.y if y is None else y
        c = self.c if c is None else c
        return {"fsdp": y, "tp": x * 2 + c}


def half_of(y, b, ny):
    return ((y - b + ny) % ny) // 2


def pick(n, table):
    out = 0
    for i, v in enumerate(table):
        if v:
            out = out + jnp.where(n == i, v, 0)
    return out


def remote(src, dst, ssem, rsem, dev):
    return pltpu.make_async_remote_copy(
        src_ref=src, dst_ref=dst, send_sem=ssem, recv_sem=rsem, device_id=dev, device_id_type=MESH
    )


def gather_logits_kernel(
    nx, ny, vocab,
    x_hbm, w_hbm, lab_hbm, xg, wo, z, sta, laba, xt,
    w, xown, xb, zb, bias, m, s, stm, xtb,
    xsend, xrecv, ysend, yrecv, wsend, wrecv, dsend, drecv, ssend, srecv, lsend, lrecv, loc, wloc, xsem, zsem, tsem,
):
    at = Place(nx, ny)
    x, y, c = at.x, at.y, at.c
    tr = xown.shape[0]
    hk = w_hbm.shape[0]
    sb = w.shape[2] // 2
    slot = NCH * sb
    left, right = (x + nx - 1) % nx, (x + 1) % nx
    top, bot = pl.ds(0, tr // 2), pl.ds(tr // 2, tr // 2)

    barrier = pltpu.get_barrier_semaphore()
    for k in range(1, nx):
        pl.semaphore_signal(barrier, inc=1, device_id=at.dev(x=(x + k) % nx), device_id_type=MESH)
    for k in range(nx):
        pl.semaphore_signal(barrier, inc=1, device_id=at.dev(x=(x + k) % nx, y=at.far), device_id_type=MESH)
    pl.semaphore_signal(barrier, inc=1, device_id=at.dev(y=at.up), device_id_type=MESH)
    pl.semaphore_signal(barrier, inc=1, device_id=at.dev(y=at.down), device_id_type=MESH)
    pl.semaphore_signal(barrier, inc=1, device_id=at.dev(c=1 - c), device_id_type=MESH)
    load_x = pltpu.make_async_copy(x_hbm, xown, loc.at[0])
    load_x.start()
    pl.semaphore_wait(barrier, 2 * nx + 2)
    load_x.wait()

    def x_send(r, to_right):
        i = 0 if to_right else 1
        src = xown if r == 0 else xg.at[1, x]
        return remote(src, xg.at[r, x], xsend.at[r, i], xrecv.at[r, i], at.dev(x=right if to_right else left))

    def x_relay(r, to_right):
        if to_right:
            part = xg.at[r, left, top]
            return remote(part, part, xsend.at[r, 2], xrecv.at[r, 2], at.dev(x=right))
        part = xg.at[r, right, bot]
        return remote(part, part, xsend.at[r, 3], xrecv.at[r, 3], at.dev(x=left))

    x_far = remote(xown, xg.at[1, x], ysend, yrecv, at.dev(y=at.far))
    keep_x = pltpu.make_async_copy(xown, xg.at[0, x], loc.at[1])

    def w_src(f, q):
        return w_hbm.at[:, pl.ds(pl.multiple_of(f * slot + q * sb, 128), sb)]

    def w_dst(k, q):
        return w.at[q, pl.ds(pl.multiple_of(k * hk, 16), hk), pl.ds(pl.multiple_of(c * sb, 128), sb)]

    def w_own(q):
        return remote(w_src(at.half, q), w_dst(y, q), wsend.at[0, q], wrecv.at[0, q], at.dev(y=at.p))

    def w_other(q):
        return remote(w_src(1 - at.half, q), w_dst(y, q), wsend.at[1, q], wrecv.at[1, q], at.dev(y=at.a))

    def w_fwd(q):
        return remote(w_dst(at.a, q), w_dst(at.a, q), wsend.at[2, q], wrecv.at[2, q], at.dev(y=at.p))

    def w_core(q):
        part = w.at[q, :, pl.ds(pl.multiple_of(c * sb, 128), sb)]
        return remote(part, part, dsend.at[q], drecv.at[q], at.dev(c=1 - c))

    def w_local(q):
        return pltpu.make_async_copy(w_src(at.half, q), w_dst(y, q), wloc.at[q])

    def w_out(q):
        w_own(q).start()
        w_other(q).start()

    w_out(0)
    x_send(0, True).start()
    x_send(0, False).start()
    keep_x.start()
    for q in range(NCH):
        w_local(q).start()

    peers = [(0, k) for k in range(1, nx)] + [(1, k) for k in range(nx)]

    def lab_copy(i):
        sy, k = peers[i]
        return remote(
            lab_hbm, laba.at[sy, x], lsend.at[i], lrecv.at[sy, x],
            at.dev(x=(x + k) % nx, y=at.far if sy else y),
        )

    for i in range(len(peers)):
        lab_copy(i).start()
    lab_own = pltpu.make_async_copy(lab_hbm, laba.at[0, x], loc.at[2])
    lab_own.start()

    col = lax.broadcasted_iota(jnp.int32, bias.shape, 1)
    row = lax.broadcasted_iota(jnp.int32, bias.shape, 0)
    b = col // sb
    pos = row * sb + col - b * sb
    half_b = jnp.where(b == 0, half_of(y, 0, ny), half_of(y, 1, ny))
    bias[...] = jnp.where((half_b == 1) & (pos >= vocab - slot), LOW, 0.0)
    m[...] = jnp.full_like(m, -3e38)
    s[...] = jnp.zeros_like(s)

    def xt_out(run, u):
        return pltpu.make_async_copy(
            xtb.at[u], xt.at[run // 2, :, pl.ds(pl.multiple_of((run % 2) * tr, 128), tr)], tsem.at[u]
        )

    w_other(0).wait_recv()
    w_fwd(0).start()
    w_out(1)
    w_other(1).wait_recv()
    w_fwd(1).start()
    w_out(2)
    keep_x.wait()
    x_send(0, True).wait_recv()
    x_relay(0, True).start()
    x_send(0, False).wait_recv()
    x_relay(0, False).start()

    n_steps = 2 * nx * NCH

    order = [(0, k, j) for k in (0, 3, 1, 2) for j in range(2)]
    order += [(0, k, 2) for k in (0, 3, 1, 2)]
    order += [(1, 0, 0), (1, 0, 1)]
    order += [(0, k, 3) for k in (0, 3, 1, 2)]
    order += [(1, 0, 2), (1, 0, 3)]
    order += [(0, k, 4) for k in (0, 3, 1, 2)]
    order += [(1, 0, 4)] + [(1, k, j) for k in (3, 1, 2) for j in range(NCH)]

    def place_of(i):
        code = pick(i, [(r * 4 + k) * 8 + j for r, k, j in order])
        run = code // 8
        return run // 4, code % 8, (x + run % 4) % nx

    def xcp(i, u):
        r, j, k = place_of(i)
        return pltpu.make_async_copy(xg.at[r, k], xb.at[u], xsem.at[u])

    def zcp(i, u):
        r, j, k = place_of(i)
        return pltpu.make_async_copy(zb.at[u], z.at[j, r, k], zsem.at[u])

    def step(i, u):
        r, j, k = place_of(i)
        run = r * nx + k
        c0 = 0
        for width in (sb * 4 // 5, 2 * sb - sb * 4 // 5) if sb % 640 == 0 else (2 * sb,):
            cols = slice(c0, c0 + width)
            zz = jnp.dot(xb[u], w[j, :, cols], preferred_element_type=F32) + bias[pl.ds(j, 1), cols]
            zb[u, :, cols] = zz
            blk = min(64, tr)
            for o in range(0, tr, blk):
                rows = slice(o, o + blk)
                m_old = m[run, rows, :]
                parts = [zz[rows, 128 * e : 128 * e + 128] for e in range(width // 128)]
                mx = m_old
                for part in parts:
                    mx = jnp.maximum(mx, part)
                acc = s[run, rows, :] * jnp.exp(m_old - mx)
                for part in parts:
                    acc = acc + jnp.exp(part - mx)
                m[run, rows, :] = mx
                s[run, rows, :] = acc
            c0 += width

    def stat_copy(r, i):
        sy, k = peers[i]
        rr = 1 - r if sy else r
        return remote(
            stm.at[r], sta.at[sy, x, rr], ssend.at[r, i], srecv.at[sy, x, rr],
            at.dev(x=(x + k) % nx, y=at.far if sy else y),
        )

    def stat_own(r):
        return pltpu.make_async_copy(stm.at[r], sta.at[0, x, r], loc.at[3 + r])

    def finish_stats(r):
        def one(d, _):
            run = r * nx + d
            mm = m[run]
            top_m = jnp.max(mm, axis=1, keepdims=True)
            tot = jnp.sum(s[run] * jnp.exp(mm - top_m), axis=1, keepdims=True)
            lane = lax.broadcasted_iota(jnp.int32, mm.shape, 1)
            blk = jnp.where(lane == 0, top_m, jnp.where(lane == 1, tot, 0.0))
            stm[r, d] = blk.T[0:8, :]
            return 0

        lax.fori_loop(0, nx, one, 0)
        for i in range(len(peers)):
            stat_copy(r, i).start()
        stat_own(r).start()

    def w_ready(j):
        w_local(j).wait()
        w_own(j).wait_recv()
        w_fwd(j).wait_recv()
        w_core(j).start()
        w_core(j).wait_recv()

    def body(t, _):
        @pl.when(t == 0)
        def _():
            for k in range(2):
                xcp(k, k).start()
            w_ready(0)
            w_ready(1)

        @pl.when(t == 2)
        def _():
            w_other(2).wait_recv()
            w_fwd(2).start()
            x_far.start()
            w_out(3)
            x_relay(0, True).wait_recv()
            x_relay(0, False).wait_recv()

        @pl.when(t == 4)
        def _():
            w_ready(2)

        @pl.when(t == 6)
        def _():
            x_far.wait_recv()
            x_send(1, True).start()
            x_send(1, False).start()
            for u in range(2):
                xcp(2 * t + u, u).start()

        @pl.when(t == 7)
        def _():
            w_other(3).wait_recv()
            w_fwd(3).start()
            w_out(4)
            w_ready(3)

        @pl.when(t == 8)
        def _():
            w_other(4).wait_recv()
            w_fwd(4).start()

        @pl.when(t == 10)
        def _():
            w_ready(4)
            pltpu.make_async_copy(w, wo, loc.at[5]).start()

        @pl.when(t == 11)
        def _():
            x_send(1, True).wait_recv()
            x_relay(1, True).start()
            x_send(1, False).wait_recv()
            x_relay(1, False).start()

        @pl.when(t == 12)
        def _():
            finish_stats(0)

        @pl.when(t == 16)
        def _():
            x_relay(1, True).wait_recv()
            x_relay(1, False).wait_recv()

        base = (t % 2) * 2
        for u in range(2):
            xcp(2 * t + u, base + u).wait()

        for u in range(2):
            r, j, k = place_of(2 * t + u)

            @pl.when(j == 0)
            def _():
                cp = xt_out(r * nx + k, u)
                xtb[u] = xb[base + u].T
                cp.start()

        @pl.when((2 * t + 2 < n_steps) & (t != 5))
        def _():
            for u in range(2):
                xcp(2 * t + 2 + u, 2 - base + u).start()

        @pl.when(t > 1)
        def _():
            for u in range(2):
                zcp(2 * t - 4 + u, base + u).wait()

        for u in range(2):
            step(2 * t + u, base + u)
        for u in range(2):
            zcp(2 * t + u, base + u).start()
            r, j, k = place_of(2 * t + u)

            @pl.when(j == 0)
            def _():
                xt_out(r * nx + k, u).wait()

        return 0

    lax.fori_loop(0, n_steps // 2, body, 0)
    finish_stats(1)
    for u in range(4):
        zcp(n_steps - 4 + u, u).wait()
    pltpu.make_async_copy(w, wo, loc.at[5]).wait()
    lab_own.wait()
    stat_own(0).wait()
    stat_own(1).wait()
    for r in range(2):
        for right_way in (True, False):
            x_send(r, right_way).wait_send()
            x_relay(r, right_way).wait_send()
    x_far.wait_send()
    for q in range(NCH):
        w_own(q).wait_send()
        w_other(q).wait_send()
        w_fwd(q).wait_send()
        w_core(q).wait_send()
    for i in range(len(peers)):
        lab_copy(i).wait_send()
        stat_copy(0, i).wait_send()
        stat_copy(1, i).wait_send()
    for sy in range(2):
        for k in range(nx):
            def arrived():
                remote(lab_hbm, laba.at[sy, k], lsend.at[0], lrecv.at[sy, k], at.dev(c=1 - c)).wait_recv()
                for rr in range(2):
                    remote(stm.at[rr], sta.at[sy, k, rr], ssend.at[0, 0], srecv.at[sy, k, rr], at.dev(c=1 - c)).wait_recv()

            if sy == 0:
                pl.when(k != x)(arrived)
            else:
                arrived()


def gather_logits(nx, ny, vocab, x, w, lab):
    tr, h = x.shape
    hk, vp = w.shape
    ch = vp // NCH
    shape = jax.ShapeDtypeStruct
    dma = pltpu.SemaphoreType.DMA
    vm = pltpu.VMEM
    flops = 2 * 2 * nx * tr * h * vp
    return pl.pallas_call(
        functools.partial(gather_logits_kernel, nx, ny, vocab),
        out_shape=(
            shape((2, nx, tr, h), BF16),
            shape((NCH, h, ch), BF16),
            shape((NCH, 2, nx, tr, ch), F32),
            shape((2, nx, 2, nx, 8, tr), F32),
            shape((2, nx) + lab.shape, jnp.int32),
            shape((nx, h, 2 * tr), BF16),
        ),
        in_specs=[ANY] * 3,
        out_specs=(ANY,) * 6,
        scratch_shapes=[
            vm((NCH, h, ch), BF16), vm((tr, h), BF16),
            vm((4, tr, h), BF16), vm((4, tr, ch), F32), vm((8, ch), F32),
            vm((2 * nx, tr, 128), F32), vm((2 * nx, tr, 128), F32), vm((2, nx, 8, tr), F32), vm((2, h, tr), BF16),
            dma((2, 4)), dma((2, 4)), dma, dma, dma((3, NCH)), dma((3, NCH)), dma((NCH,)), dma((NCH,)),
            dma((2, 2 * nx - 1)), dma((2, nx, 2)), dma((2 * nx - 1,)), dma((2, nx)),
            dma((6,)), dma((NCH,)), dma((4,)), dma((4,)), dma((2,)),
        ],
        compiler_params=pltpu.CompilerParams(
            collective_id=0, has_side_effects=True, vmem_limit_bytes=60 * 2**20
        ),
        cost_estimate=pl.CostEstimate(flops=flops, bytes_accessed=4 * 2 * nx * tr * vp, transcendentals=0),
        name="gather_logits",
    )(x, w, lab)


def grads_kernel(
    nx, ny, inv, z, w_hbm, xt_hbm, st8, dxo, dwo, loss, rx, fx, dd, rr,
    w, xt, zb, gb, acc, dx, st, lacc, tmpa, tmpb, keep, fin, fdx, lbuf,
    wsem, tsem, zsem, xsend, xrecv, fsend, frecv, dsend, drecv, rsend, rrecv, osend, orecv, asem, bsem, lsend, lrecv,
    out_sem,
):
    at = Place(nx, ny)
    x, y, c = at.x, at.y, at.c
    tr, h = dxo.shape
    ch = zb.shape[2]
    sb = ch // 2
    slot = NCH * sb
    hk = dwo.shape[0]
    nq = rx.shape[2]
    qr = tr // nq
    left, right = (x + nx - 1) % nx, (x + 1) % nx

    def par(yy, b):
        return jnp.where((yy + b) % 2 == 0, (yy + 1) % ny, (yy + ny - 1) % ny)

    def adj(yy, b):
        return jnp.where((yy + b) % 2 == 0, (yy + ny - 1) % ny, (yy + 1) % ny)

    for j in range(NCH):
        pltpu.make_async_copy(w_hbm.at[j], w.at[j], wsem.at[j]).start()
    barrier = pltpu.get_barrier_semaphore()
    for k in range(1, nx):
        pl.semaphore_signal(barrier, inc=1, device_id=at.dev(x=(x + k) % nx), device_id_type=MESH)
    for k in range(1, ny):
        pl.semaphore_signal(barrier, inc=1, device_id=at.dev(y=(y + k) % ny), device_id_type=MESH)
        pl.semaphore_signal(barrier, inc=1, device_id=at.dev(y=(y + k) % ny, c=1 - c), device_id_type=MESH)
    pl.semaphore_signal(barrier, inc=1, device_id=at.dev(c=1 - c), device_id_type=MESH)

    segments = ["x0", "w0", "w1", "x1", "w2", "w3", "x2", "w4", "x3"]
    bodies = []
    for seg in segments:
        for k in range(NCH if seg[0] == "x" else nx):
            bodies.append((0 if seg[0] == "x" else 1, int(seg[1]), k))
    n_body = len(bodies)
    first = {seg: bodies.index((0 if seg[0] == "x" else 1, int(seg[1]), 0)) for seg in segments}
    after = {seg: first[seg] + (NCH if seg[0] == "x" else nx) for seg in segments}

    def body_at(n):
        return pick(n, [b[0] for b in bodies]), pick(n, [b[1] for b in bodies]), pick(n, [b[2] for b in bodies])

    def tile(n, u):
        kind, i, k = body_at(n)
        mine = jnp.where(u == 0, (x + 2 * nx - 1 - i) % nx, (x + 1 + i) % nx)
        run = 2 * k + u
        is_x = kind == 0
        return jnp.where(is_x, k, i), jnp.where(is_x, u, run // nx), jnp.where(is_x, mine, run % nx)

    def zcp(n, u, buf):
        j, r, d = tile(n, u)
        return pltpu.make_async_copy(z.at[j, r, d], zb.at[buf], zsem.at[buf])

    for u in range(2):
        zcp(0, u, u).start()
    pltpu.make_async_copy(xt_hbm, xt, tsem).start()

    def spread(run, _):
        st[run] = jnp.concatenate([st8[run // nx, run % nx]] * 16, axis=0).T
        return 0

    lax.fori_loop(0, 2 * nx, spread, 0)
    lacc[...] = jnp.zeros_like(lacc)
    pl.semaphore_wait(barrier, nx - 1 + 2 * (ny - 1) + 1)

    def x_copy(s, dr, q):
        return remote(
            dx.at[s % 2, dr, pl.ds(pl.multiple_of(q * qr, 8), qr)], rx.at[s, dr, q],
            xsend.at[s, dr, q], xrecv.at[s, dr, q], at.dev(x=left if dr else right),
        )

    def far_copy(q):
        return remote(
            dx.at[1, 1, pl.ds(pl.multiple_of(q * qr, 8), qr)], fx.at[q], fsend.at[q], frecv.at[q], at.dev(y=at.far)
        )

    def a_load(s, q, dr):
        return pltpu.make_async_copy(rx.at[s - 1, dr, q], tmpa.at[q % 2, dr], asem.at[q % 2, dr])

    def a_pre(s, q):
        for dr in range(2):
            x_copy(s - 1, dr, q).wait_recv()
            a_load(s, q, dr).start()

    def a_use(s, q):
        rows = pl.ds(pl.multiple_of(q * qr, 8), qr)
        for dr in range(2):
            a_load(s, q, dr).wait()
            dx[s % 2, dr, rows, :] += tmpa[q % 2, dr]

        @pl.when(s < nx - 1)
        def _():
            for dr in range(2):
                x_copy(s, dr, q).start()

        @pl.when(s == nx - 1)
        def _():
            far_copy(q).start()

    def f_load(q):
        return pltpu.make_async_copy(fx.at[q], tmpa.at[q % 2, 0], asem.at[q % 2, 0])

    def f_out(q):
        return pltpu.make_async_copy(fdx.at[q % 2], dxo.at[pl.ds(pl.multiple_of(q * qr, 16), qr)], out_sem.at[q])

    def f_pre(q):
        far_copy(q).wait_recv()
        f_load(q).start()

    def f_use(q):
        f_load(q).wait()

        @pl.when(q > 1)
        def _():
            f_out(q - 2).wait()

        rows = pl.ds(pl.multiple_of(q * qr, 8), qr)
        fdx[q % 2] = (dx[1, 0, rows, :] + tmpa[q % 2, 0]).astype(BF16)
        f_out(q).start()

    def lot(b):
        q = (c + b) % 2
        slices = [(b + 2 * q) % ny, (b + 1 + 2 * q) % ny]
        other = [(b + 2 * (1 - q)) % ny, (b + 1 + 2 * (1 - q)) % ny]
        home = half_of(y, b, ny) == q
        kt = jnp.where(home, y, adj(y, b))
        it = jnp.where(slices[0] == kt, 0, 1)
        return slices, other, kt, it, home

    def rows_of(k):
        return pl.ds(pl.multiple_of(k * hk, 16), hk)

    def d_copy(j, b, i):
        other = lot(b)[1]
        return remote(
            acc.at[j % 2, rows_of(other[i]), pl.ds(b * sb, sb)], dd.at[j, b, i],
            dsend.at[j, b, i], drecv.at[j, b, i], at.dev(c=1 - c),
        )

    def d_send(j):
        for b in range(2):
            for i in range(2):
                d_copy(j, b, i).start()

    def r_load(j, b, i):
        return pltpu.make_async_copy(dd.at[j, b, i], tmpb.at[b, i], bsem.at[b, i])

    def r_pre(j):
        for b in range(2):
            for i in range(2):
                d_copy(j, b, i).wait_recv()
                r_load(j, b, i).start()

    def r_copy(j, b):
        slices, _, _, it, _ = lot(b)
        kg = jnp.where(it == 0, slices[1], slices[0])
        src = acc.at[j % 2, rows_of(kg), pl.ds(b * sb, sb)]
        return remote(src, rr.at[j, b], rsend.at[j, b], rrecv.at[j, b], at.dev(y=par(y, b)))

    def r_use(j):
        for b in range(2):
            slices, _, kt, it, _ = lot(b)
            kg = jnp.where(it == 0, slices[1], slices[0])
            for i in range(2):
                r_load(j, b, i).wait()

            acc[j % 2, rows_of(kg), pl.ds(b * sb, sb)] += tmpb[b, 1 - it]
            r_copy(j, b).start()
            keep[j % 2, b] = acc[j % 2, rows_of(kt), pl.ds(b * sb, sb)] + tmpb[b, it]

    def s_load(j, b):
        return pltpu.make_async_copy(rr.at[j, b], tmpb.at[b, 0], bsem.at[b, 0])

    def s_pre(j):
        for b in range(2):
            r_copy(j, b).wait_recv()
            s_load(j, b).start()

    def o_copy(j, b):
        kt = lot(b)[2]
        f = half_of(y, b, ny)
        dst = dwo.at[:, pl.ds(pl.multiple_of(f * slot + j * sb, 128), sb)]
        return remote(fin.at[b], dst, osend.at[j, b], orecv.at[f, j], at.dev(y=kt, c=b))

    def o_here(j, b):
        f = half_of(y, b, ny)
        dst = dwo.at[:, pl.ds(pl.multiple_of(f * slot + j * sb, 128), sb)]
        return pltpu.make_async_copy(fin.at[b], dst, orecv.at[f, j])

    def is_here(b):
        return lot(b)[4] & (c == b)

    def s_use(j):
        for b in range(2):
            s_load(j, b).wait()

            @pl.when((j > 0) & jnp.logical_not(is_here(b)))
            def _():
                o_copy(j - 1, b).wait_send()

            @pl.when((j > 0) & is_here(b))
            def _():
                o_here(j - 1, b).wait()

            fin[b] = (keep[j % 2, b] + tmpb[b, 0]).astype(BF16)

            @pl.when(is_here(b))
            def _():
                o_here(j, b).start()

            @pl.when(jnp.logical_not(is_here(b)))
            def _():
                o_copy(j, b).start()

    def l_copy(stage, k):
        if stage == 0:
            return remote(lbuf.at[0, x], lbuf.at[0, x], lsend.at[0, k], lrecv.at[0, x], at.dev(x=(x + k) % nx))
        if stage == 1:
            return remote(lbuf.at[1, y], lbuf.at[1, y], lsend.at[1, k], lrecv.at[1, y], at.dev(y=(y + k) % ny))
        return remote(lbuf.at[2, c], lbuf.at[2, c], lsend.at[2, 0], lrecv.at[2, c], at.dev(c=1 - c))

    def l_sum(stage, size, me):
        for k in range(size):
            @pl.when(k != me)
            def _():
                remote(
                    lbuf.at[stage, k], lbuf.at[stage, k], lsend.at[stage, 0], lrecv.at[stage, k], at.dev(c=1 - c)
                ).wait_recv()

        total = lbuf[stage, 0]
        for k in range(1, size):
            total = total + lbuf[stage, k]
        return total

    def l_start():
        mine = -jnp.sum(lacc[...].reshape(-1, 8, 128), axis=0)
        logs = st8[0, x, 3:4, :]
        for o in range(tr // 128):
            mine = mine + jnp.concatenate([logs[:, 128 * o : 128 * o + 128], jnp.zeros((7, 128), F32)], axis=0)
        lbuf[0, x] = mine
        for k in range(1, nx):
            l_copy(0, k).start()

    def l_mid():
        lbuf[1, y] = l_sum(0, nx, x)
        for k in range(1, ny):
            l_copy(1, k).start()

    def l_late():
        lbuf[2, c] = l_sum(1, ny, y)
        l_copy(2, 0).start()

    def make_g(n, u, buf, c0, c1, want_loss):
        j, r, d = tile(n, u)
        run = r * nx + d
        blk = min(64, tr)
        for o in range(0, tr, blk):
            rows = slice(o, o + blk)
            t = st[run, rows, :]
            top = jnp.broadcast_to(t[:, 0:1], (blk, 128))
            scale = jnp.broadcast_to(t[:, 1:2], (blk, 128))
            lab = jnp.broadcast_to(t[:, 2:3], (blk, 128)).astype(jnp.int32) - j * ch
            lane = lax.broadcasted_iota(jnp.int32, (blk, 128), 1)
            add = jnp.zeros((blk, 128), F32)
            for e in range(c0 // 128, c1 // 128):
                cols = slice(128 * e, 128 * e + 128)
                dist = zb[buf, rows, cols] - top
                g = jnp.exp(dist) * scale
                hit = lab - 128 * e == lane
                if want_loss:
                    add = add + jnp.where(hit, dist, 0.0)
                gb[u, rows, cols] = jnp.where(hit, g - inv, g).astype(BF16)
            if want_loss:
                lacc[...] += add

    x_cuts = [(0, ch * 2 // 5), (ch * 2 // 5, ch)] if ch % 640 == 0 else [(0, ch)]
    w_cuts = [(0, ch // 5), (ch // 5, ch * 3 // 5), (ch * 3 // 5, ch)] if ch % 1280 == 0 else [(0, ch)]

    def x_body(n, base):
        _, s, j = body_at(n)
        half = s % 2

        @pl.when(j == 0)
        def _():
            dx[half] = jnp.zeros(dx.shape[1:], F32)

        for u in range(2):
            for c0, c1 in x_cuts:
                make_g(n, u, base + u, c0, c1, True)
                dx[half, u] += lax.dot_general(
                    gb[u, :, c0:c1], w[j, :, c0:c1], (((1,), (1,)), ((), ())), preferred_element_type=F32
                )

    def w_body(n, base):
        _, j, k = body_at(n)
        half = j % 2

        @pl.when(k == 0)
        def _():
            acc[half] = jnp.zeros(acc.shape[1:], F32)

        for c0, c1 in w_cuts:
            for u in range(2):
                make_g(n, u, base + u, c0, c1, False)
            acc[half, :, c0:c1] += jnp.dot(
                xt[k], gb[:, :, c0:c1].reshape(2 * tr, c1 - c0), preferred_element_type=F32
            )

    last = n_body
    plan_a = [(after["x1"] + q, 1, q) for q in range(nq)] + [(after["x2"] + q, 2, q) for q in range(nq)]
    plan_a += [(last + q, 3, q) for q in range(nq)]
    plan_r = [(11, 12, 0), (15, 17, 1), (24, 25, 2), (28, 30, 3), (37, 38, 4)]
    plan_s = [(18, 19, 0), (22, 23, 1), (31, 32, 2), (35, 36, 3), (last + 1, last + 2, 4)]
    plan_f = [(last + nq + q, q) for q in range(nq)]
    n_all = last + 2 * nq

    def when(n, table, fn):
        table = [(e[0], e[1:]) for e in table]
        hit = functools.reduce(lambda p, q: p | q, [n == e for e, _ in table])

        @pl.when(hit)
        def _():
            args = []
            for i in range(len(table[0][1])):
                val = 0
                for e, vals in table:
                    if vals[i]:
                        val = val + jnp.where(n == e, vals[i], 0)
                args.append(val + jnp.int32(0))
            fn(*args)

    def body(n, _):
        @pl.when(n < NCH)
        def _():
            pltpu.make_async_copy(w_hbm.at[n], w.at[n], wsem.at[n]).wait()

        @pl.when(n == first["w0"])
        def _():
            pltpu.make_async_copy(xt_hbm, xt, tsem).wait()
            for q in range(nq):
                for dr in range(2):
                    x_copy(0, dr, q).start()

        when(n, [(after["w%d" % j], j) for j in range(NCH)], d_send)
        when(n, plan_a, a_use)
        when(n, plan_f, f_use)
        when(n, [(e[1], e[2]) for e in plan_r], r_use)
        when(n, [(e[1], e[2]) for e in plan_s], s_use)
        when(n, [(e[0] - 1,) + e[1:] for e in plan_a], a_pre)
        when(n, [(e[0] - 1,) + e[1:] for e in plan_f], f_pre)
        when(n, [(e[0], e[2]) for e in plan_r], r_pre)
        when(n, [(e[0], e[2]) for e in plan_s], s_pre)

        @pl.when(n == last)
        def _():
            l_start()

        @pl.when(n == last + 2)
        def _():
            l_mid()

        @pl.when(n == last + nq + 1)
        def _():
            l_late()

        @pl.when((n == first["x2"]) | (n == first["x3"]))
        def _():
            s = jnp.where(n == first["x2"], 0, 1)
            for q in range(nq):
                for dr in range(2):
                    x_copy(s, dr, q).wait_send()

        for j in range(2, NCH):
            @pl.when(n == first["w%d" % j])
            def _():
                for b in range(2):
                    r_copy(j - 2, b).wait_send()
                    for i in range(2):
                        d_copy(j - 2, b, i).wait_send()

        base = (n % 2) * 2

        @pl.when(n < n_body)
        def _():
            for u in range(2):
                zcp(n, u, base + u).wait()

            @pl.when(n + 1 < n_body)
            def _():
                for u in range(2):
                    zcp(n + 1, u, 2 - base + u).start()

            kind = body_at(n)[0]

            @pl.when(kind == 0)
            def _():
                x_body(n, base)

            @pl.when(kind == 1)
            def _():
                w_body(n, base)

        return 0

    lax.fori_loop(0, n_all, body, 0)
    loss[...] = l_sum(2, 2, c)

    for q in range(nq):
        if q >= nq - 2:
            f_out(q).wait()
        far_copy(q).wait_send()
        for dr in range(2):
            x_copy(2, dr, q).wait_send()
    for b in range(2):
        for j in range(NCH - 2, NCH):
            for i in range(2):
                d_copy(j, b, i).wait_send()
            r_copy(j, b).wait_send()

        @pl.when(is_here(b))
        def _():
            o_here(NCH - 1, b).wait()

        @pl.when(jnp.logical_not(is_here(b)))
        def _():
            o_copy(NCH - 1, b).wait_send()

    q0 = half_of(y, c, ny)
    for f in range(2):
        local = (f == q0) & ((q0 + c) % 2 == c)

        @pl.when(jnp.logical_not(local))
        def _():
            for j in range(NCH):
                dst = dwo.at[:, pl.ds(f * slot + j * sb, sb)]
                remote(fin.at[0], dst, osend.at[j, 0], orecv.at[f, j], at.dev(c=1 - c)).wait_recv()

    for k in range(1, nx):
        l_copy(0, k).wait_send()
    for k in range(1, ny):
        l_copy(1, k).wait_send()
    l_copy(2, 0).wait_send()


def grads(nx, ny, inv, z, w, xt, st8, hk):
    h = w.shape[1]
    ch = w.shape[2]
    tr = z.shape[3]
    nq = 4
    shape = jax.ShapeDtypeStruct
    dma = pltpu.SemaphoreType.DMA
    vm = pltpu.VMEM
    vspec = pl.BlockSpec(memory_space=pltpu.VMEM)
    sb, qr = ch // 2, tr // nq
    return pl.pallas_call(
        functools.partial(grads_kernel, nx, ny, inv),
        out_shape=(
            shape((tr, h), BF16), shape((hk, NCH * ch), BF16), shape((8, 128), F32),
            shape((nx - 1, 2, nq, qr, h), F32), shape((nq, qr, h), F32),
            shape((NCH, 2, 2, hk, sb), F32), shape((NCH, 2, hk, sb), F32),
        ),
        in_specs=[ANY, ANY, ANY, vspec],
        out_specs=(ANY, ANY, vspec, ANY, ANY, ANY, ANY),
        scratch_shapes=[
            vm((NCH, h, ch), BF16), vm((nx, h, 2 * tr), BF16), vm((4, tr, ch), F32), vm((2, tr, ch), BF16),
            vm((2, h, ch), F32), vm((2, 2, tr, h), F32), vm((2 * nx, tr, 128), F32), vm((min(64, tr), 128), F32),
            vm((2, 2, qr, h), F32), vm((2, 2, hk, sb), F32), vm((2, 2, hk, sb), F32),
            vm((2, hk, sb), BF16), vm((2, qr, h), BF16), vm((3, max(nx, ny), 8, 128), F32),
            dma((NCH,)), dma, dma((4,)), dma((nx - 1, 2, nq)), dma((nx - 1, 2, nq)), dma((nq,)), dma((nq,)),
            dma((NCH, 2, 2)), dma((NCH, 2, 2)), dma((NCH, 2)), dma((NCH, 2)), dma((NCH, 2)), dma((2, NCH)),
            dma((2, 2)), dma((2, 2)), dma((3, max(nx, ny))), dma((3, max(nx, ny))), dma((nq,)),
        ],
        compiler_params=pltpu.CompilerParams(
            collective_id=1, has_side_effects=True, vmem_limit_bytes=67_000_000
        ),
        name="grads",
    )(z, w, xt, st8)


def solution(mesh):
    ny = mesh.shape["fsdp"]
    tp_size = mesh.shape["tp"]
    nx = tp_size // 2
    token_spec = P(("dp", "fsdp", "tp"), None)
    label_spec = P(("dp", "fsdp", "tp"))

    def local_step(hidden, w_head, labels):
        tr, h = hidden.shape
        hk, vocab = w_head.shape
        inv = 1.0 / (tr * tp_size * ny)
        vp = -(-vocab // (256 * NCH)) * (256 * NCH)
        ch = vp // NCH
        sb = ch // 2
        slot = NCH * sb
        tp = lax.axis_index("tp")
        x, y = tp // 2, lax.axis_index("fsdp")
        w_pad = jnp.pad(w_head, ((0, 0), (0, vp - vocab)))
        lab8 = jnp.pad(labels.reshape(-1, 128), ((0, 8 - tr // 128), (0, 0)))
        xg, wg, z, sta, laba, xt = gather_logits(nx, ny, vocab, hidden, w_pad, lab8)

        ms = sta[..., 0, :].reshape(2 * nx, 2, nx, tr)
        ss = sta[..., 1, :].reshape(2 * nx, 2, nx, tr)
        top = jnp.max(ms, axis=0)
        tot = jnp.sum(ss * jnp.exp(ms - top), axis=0)
        lab = laba[:, :, 0 : tr // 128, :].reshape(2, nx, tr)
        shard, off = lab // vocab, lab % vocab
        b, f = shard % 2, off // slot
        pos = off - f * slot
        mine = (shard // 2 == x) & (half_of(y, b, ny) == f)
        col = jnp.where(mine, (pos // sb) * ch + b * sb + pos % sb, -1)
        rows = [top, inv / tot, col.astype(F32), jnp.log(tot)]
        st8 = jnp.stack(rows + [jnp.zeros_like(top)] * 4, axis=2)
        d_hidden, d_w, loss = grads(nx, ny, inv, z, wg, xt, st8, hk)[:3]
        mean_loss = jnp.sum(loss) * inv
        return mean_loss.reshape(1), d_hidden, d_w[:, :vocab]

    return jax.shard_map(
        local_step,
        mesh=mesh,
        in_specs=(token_spec, P("fsdp", "tp"), label_spec),
        out_specs=(P("dp"), token_spec, P(("dp", "fsdp"), "tp")),
        check_vma=False,
    )
```

time: 1030 us -> 451 us (0.44)
  the two profiles are of different devices: /device:TPU:97 before, /device:TPU:111 now
where the time goes in v2:
time: 451 us; the launch traced here: 450 us
  Pallas kernels  426 us (94%)
  local copies, waits for them, and re-layouts  14.6 us (3%)
  other arithmetic  6.72 us (1%)
    pallas_call x1, Pallas kernels, grads(): pl.pallas_call(functools.partial(grads_kernel, nx, ny, inv), out_shape=(s...  266 us
    pallas_call x1, Pallas kernels, gather_logits(): pl.pallas_call(functools.partial(gather_logits_kernel, nx, ny, vocab), ou...  160 us
    unnamed x5, local copies, waits for them, and re-layouts  10.6 us

profile of v2, /device:TPU:111, one launch (start us, length us, event | category | flops | bytes accessed | tf_op | source)
XLA Modules:
  0.0 449.9 jit_solution(17225458560874373930)
XLA Ops:
  0.6 1.3 pad.9.lab_hbm
  1.9 4.0 copy.9
  5.9 1.9 pad.8.w_hbm
  7.8 159.6 %gather_logits.1 = (bf16[2,4,512,1024]{3,2,1,0:T(8,128)(2,1)}, bf16[5,1024,1280]{2,1,0:T(8,128)(2,1)}, f32[5,2,4,512,1280]{4,3,2,1,0:T(8,128)}, f32[2,4,2,4,8,51...) custom-call(bf16[512,1024]{1,0:T(8,128)(2,1)} %x_hbm.1, bf16[256,6400]{1,0:T(8,128)(2,1)} %pad.8.w_hbm, ...), custom_call_target="tpu_custom_call" | custom-call | flops 53687091200 | bytes 104857600 | tf_op jit(solution)/shard_map/gather_logits/pallas_call | solution.py:392
  167.4 0.8 sign_compare_fusion
  168.2 0.8 slice_divide_fusion
  169.0 0.6 fusion.2
  169.6 1.4 slice_reduce_fusion
  171.0 1.9 multiply_reduce_fusion
  172.9 0.8 stack.14.st8
  173.7 266.5 %grads.1 = (bf16[512,1024]{1,0:T(8,128)(2,1)}, bf16[256,6400]{1,0:T(8,128)(2,1)}, f32[8,128]{1,0:T(8,128)}, f32[3,2,4,128,1024]{4,3,2,1,0:T(8,128)}, f32[4,128,1...) custom-call(f32[5,2,4,512,1280]{4,3,2,1,0:T(8,128)} %get-tuple-element.11.z, ...), custom_call_target="tpu_custom_call" | custom-call | tf_op jit(solution)/shard_map/grads/pallas_call | solution.py:877
  440.2 0.0 copy-start
  440.2 1.4 reduce_sum.19
  442.2 5.6 %copy.12 = bf16[256,6288]{0,1:T(8,128)(2,1)} copy(bf16[256,6288]{1,0:T(8,128)(2,1)} %bitcast.7) | data formatting | bytes 6438912
  447.8 0.0 copy-done
  447.8 1.0 copy.14
  (6 shorter events, 0.1 us)
Async XLA Ops:
  440.2 7.6 %copy-start = (bf16[512,1024]{1,0:T(8,128)(2,1)S(1)}, bf16[512,1024]{1,0:T(8,128)(2,1)}, u32[]{:S(2)}) copy-start(bf16[512,1024]{1,0:T(8,128)(2,1)} %get-tuple-element.33) | copy-start | bytes 3145732

commit v3 on v2

v3 whole, which is shorter than its diff:
```python
import functools

import jax
import jax.numpy as jnp
from jax import lax
from jax.experimental import pallas as pl
from jax.experimental.pallas import tpu as pltpu
from jax.sharding import PartitionSpec as P

MESH = pl.DeviceIdType.MESH
F32 = jnp.float32
BF16 = jnp.bfloat16
NCH = 5
LOW = -1e30
ANY = pl.BlockSpec(memory_space=pl.ANY)
LANES = 128
SUB = 8
TWO = 2
BOTH = range(TWO)
RIGHT, LEFT = True, False


class Place:
    def __init__(self, nx, ny):
        tp = lax.axis_index("tp")
        self.nx, self.ny = nx, ny
        self.x, self.c, self.y = tp // TWO, tp % TWO, lax.axis_index("fsdp")
        up, down = (self.y + 1) % ny, (self.y + ny - 1) % ny
        even = (self.y + self.c) % TWO == 0
        self.up, self.down = up, down
        self.pc = 1 - self.c
        self.p = jnp.where(even, up, down)
        self.a = jnp.where(even, down, up)
        self.far = (self.y + 2) % ny
        self.half = ((self.y - self.c + ny) % ny) // TWO

    def dev(self, x=None, y=None, c=None):
        x = self.x if x is None else x
        y = self.y if y is None else y
        c = self.c if c is None else c
        return {"fsdp": y, "tp": x * 2 + c}


def half_of(y, b, ny):
    return ((y - b + ny) % ny) // TWO


def pick(n, table):
    out = 0
    for i, v in enumerate(table):
        if v:
            out = out + jnp.where(n == i, v, 0)
    return out


def remote(src, dst, ssem, rsem, dev):
    return pltpu.make_async_remote_copy(
        src_ref=src, dst_ref=dst, send_sem=ssem, recv_sem=rsem, device_id=dev, device_id_type=MESH
    )


def local(src, dst, sem):
    return pltpu.make_async_copy(src, dst, sem)


def gather_logits_kernel(
    nx, ny, vocab,
    x_hbm, w_hbm, lab_hbm, xg, wo, z, sta, laba, xt,
    w, xown, xb, zb, bias, m, s, stm, xtb,
    xsend, xrecv, ysend, yrecv, wsend, wrecv, dsend, drecv, ssend, srecv, lsend, lrecv, loc, wloc, xsem, zsem, tsem,
):
    at = Place(nx, ny)
    x, y, c = at.x, at.y, at.c
    tr = xown.shape[0]
    hk = w_hbm.shape[0]
    sb = w.shape[2] // TWO
    slot = NCH * sb
    left, right = (x + nx - 1) % nx, (x + 1) % nx
    top, bot = pl.ds(0, tr // TWO), pl.ds(tr // TWO, tr // TWO)

    barrier = pltpu.get_barrier_semaphore()
    for k in range(1, nx):
        pl.semaphore_signal(barrier, inc=1, device_id=at.dev(x=(x + k) % nx), device_id_type=MESH)
    for k in range(nx):
        pl.semaphore_signal(barrier, inc=1, device_id=at.dev(x=(x + k) % nx, y=at.far), device_id_type=MESH)
    pl.semaphore_signal(barrier, inc=1, device_id=at.dev(y=at.up), device_id_type=MESH)
    pl.semaphore_signal(barrier, inc=1, device_id=at.dev(y=at.down), device_id_type=MESH)
    pl.semaphore_signal(barrier, inc=1, device_id=at.dev(c=at.pc), device_id_type=MESH)
    load_x = local(x_hbm, xown, loc.at[0])
    load_x.start()
    pl.semaphore_wait(barrier, TWO * nx + 2)
    load_x.wait()

    def x_send(r, to_right):
        i = 0 if to_right else 1
        src = xown if r == 0 else xg.at[1, x]
        return remote(src, xg.at[r, x], xsend.at[r, i], xrecv.at[r, i], at.dev(x=right if to_right else left))

    def x_relay(r, to_right):
        if to_right:
            part = xg.at[r, left, top]
            return remote(part, part, xsend.at[r, 2], xrecv.at[r, 2], at.dev(x=right))
        part = xg.at[r, right, bot]
        return remote(part, part, xsend.at[r, 3], xrecv.at[r, 3], at.dev(x=left))

    x_far = remote(xown, xg.at[1, x], ysend, yrecv, at.dev(y=at.far))
    keep_x = local(xown, xg.at[0, x], loc.at[1])

    def w_src(f, q):
        return w_hbm.at[:, pl.ds(pl.multiple_of(f * slot + q * sb, LANES), sb)]

    def w_dst(k, q):
        return w.at[q, pl.ds(pl.multiple_of(k * hk, 16), hk), pl.ds(pl.multiple_of(c * sb, LANES), sb)]

    def w_own(q):
        return remote(w_src(at.half, q), w_dst(y, q), wsend.at[0, q], wrecv.at[0, q], at.dev(y=at.p))

    def w_other(q):
        return remote(w_src(1 - at.half, q), w_dst(y, q), wsend.at[1, q], wrecv.at[1, q], at.dev(y=at.a))

    def w_fwd(q):
        return remote(w_dst(at.a, q), w_dst(at.a, q), wsend.at[2, q], wrecv.at[2, q], at.dev(y=at.p))

    def w_core(q):
        part = w.at[q, :, pl.ds(pl.multiple_of(c * sb, LANES), sb)]
        return remote(part, part, dsend.at[q], drecv.at[q], at.dev(c=at.pc))

    def w_local(q):
        return local(w_src(at.half, q), w_dst(y, q), wloc.at[q])

    def w_out(q):
        w_own(q).start()
        w_other(q).start()

    w_out(0)
    x_send(0, RIGHT).start()
    x_send(0, LEFT).start()
    keep_x.start()
    for q in range(NCH):
        w_local(q).start()

    peers = [(0, k) for k in range(1, nx)] + [(1, k) for k in range(nx)]

    def lab_copy(i):
        sy, k = peers[i]
        return remote(
            lab_hbm, laba.at[sy, x], lsend.at[i], lrecv.at[sy, x],
            at.dev(x=(x + k) % nx, y=at.far if sy else y),
        )

    for i in range(len(peers)):
        lab_copy(i).start()
    lab_own = local(lab_hbm, laba.at[0, x], loc.at[2])
    lab_own.start()

    tail = lax.broadcasted_iota(jnp.int32, bias.shape[1:], 1)
    slot_of = tail // LANES
    pos = slot - LANES + tail - slot_of * LANES
    half_b = jnp.where(slot_of == 0, half_of(y, 0, ny), half_of(y, 1, ny))
    bias[...] = jnp.zeros_like(bias)
    bias[NCH - 1] = jnp.where((half_b == 1) & (pos >= vocab - slot), LOW, 0.0)
    m[...] = jnp.full_like(m, -3e38)
    s[...] = jnp.zeros_like(s)

    def xt_out(run, u):
        return local(
            xtb.at[u], xt.at[run // TWO, :, pl.ds(pl.multiple_of((run % TWO) * tr, LANES), tr)], tsem.at[u]
        )

    w_other(0).wait_recv()
    w_fwd(0).start()
    w_out(1)
    w_other(1).wait_recv()
    w_fwd(1).start()
    w_out(2)
    keep_x.wait()
    x_send(0, RIGHT).wait_recv()
    x_relay(0, RIGHT).start()
    x_send(0, LEFT).wait_recv()
    x_relay(0, LEFT).start()

    n_steps = TWO * nx * NCH

    order = [(0, k, j) for k in (0, 3, 1, TWO) for j in BOTH]
    order += [(0, k, TWO) for k in (0, 3, 1, TWO)]
    order += [(1, 0, 0), (1, 0, 1)]
    order += [(0, k, 3) for k in (0, 3, 1, TWO)]
    order += [(1, 0, TWO), (1, 0, 3)]
    order += [(0, k, 4) for k in (0, 3, 1, TWO)]
    order += [(1, 0, 4)] + [(1, k, j) for k in (3, 1, TWO) for j in range(NCH)]

    codes = [(r * 4 + k) * 8 + j for r, k, j in order]

    def code_of(t):
        return tuple(pick(t, codes[u::TWO]) for u in BOTH)

    def place_of(code):
        run = code // 8
        return run // 4, code % 8, (x + run % 4) % nx

    def xcp(i, u):
        r, j, k = place_of(i)
        return local(xg.at[r, k], xb.at[u], xsem.at[u])

    def zcp(i, u):
        r, j, k = place_of(i)
        return local(zb.at[u], z.at[j, r, k], zsem.at[u])

    def step(i, u):
        r, j, k = place_of(i)
        run = r * nx + k
        c0 = 0
        for width in (sb * 4 // 5, TWO * sb - sb * 4 // 5) if sb % 640 == 0 else (2 * sb,):
            cols = slice(c0, c0 + width)
            zz = jnp.dot(xb[u], w[j, :, cols], preferred_element_type=F32)
            zb[u, :, cols] = zz
            blk = min(64, tr)
            for o in range(0, tr, blk):
                rows = slice(o, o + blk)
                m_old = m[run, rows, :]
                parts = [zz[rows, LANES * e : LANES * e + LANES] for e in range(width // LANES)]
                for e in range(width // LANES):
                    at_e = slice(c0 + LANES * e, c0 + LANES * e + LANES)
                    if at_e.stop % sb == 0:
                        end = at_e.stop // sb
                        parts[e] = parts[e] + bias[j, 0:1, LANES * end - LANES : LANES * end]
                        zb[u, rows, at_e] = parts[e]
                mx = m_old
                for part in parts:
                    mx = jnp.maximum(mx, part)
                acc = s[run, rows, :] * jnp.exp(m_old - mx)
                for part in parts:
                    acc = acc + jnp.exp(part - mx)
                m[run, rows, :] = mx
                s[run, rows, :] = acc
            c0 += width

    def stat_copy(r, i):
        sy, k = peers[i]
        rr = 1 - r if sy else r
        return remote(
            stm.at[r], sta.at[sy, x, rr], ssend.at[r, i], srecv.at[sy, x, rr],
            at.dev(x=(x + k) % nx, y=at.far if sy else y),
        )

    def stat_own(r):
        return local(stm.at[r], sta.at[0, x, r], loc.at[3 + r])

    def finish_stats(r):
        def one(d, _):
            run = r * nx + d
            mm = m[run]
            top_m = jnp.max(mm, axis=1, keepdims=True)
            tot = jnp.sum(s[run] * jnp.exp(mm - top_m), axis=1, keepdims=True)
            lane = lax.broadcasted_iota(jnp.int32, mm.shape, 1)
            blk = jnp.where(lane == 0, top_m, jnp.where(lane == 1, tot, 0.0))
            stm[r, d] = blk.T[0:SUB, :]
            return 0

        lax.fori_loop(0, nx, one, 0)
        for i in range(len(peers)):
            stat_copy(r, i).start()
        stat_own(r).start()

    def w_ready(j):
        w_local(j).wait()
        w_own(j).wait_recv()
        w_fwd(j).wait_recv()
        w_core(j).start()
        w_core(j).wait_recv()

    def body(t, held):
        older, old, now = held
        later = code_of(t + 1)

        @pl.when(t == 0)
        def _():
            for u in BOTH:
                xcp(now[u], u).start()
            w_ready(0)
            w_ready(1)

        @pl.when(t == 2)
        def _():
            w_other(2).wait_recv()
            w_fwd(2).start()
            x_far.start()
            w_out(3)
            x_relay(0, RIGHT).wait_recv()
            x_relay(0, LEFT).wait_recv()

        @pl.when(t == 4)
        def _():
            w_ready(2)

        @pl.when(t == 6)
        def _():
            x_far.wait_recv()
            x_send(1, RIGHT).start()
            x_send(1, LEFT).start()
            for u in BOTH:
                xcp(now[u], u).start()

        @pl.when(t == 7)
        def _():
            w_other(3).wait_recv()
            w_fwd(3).start()
            w_out(4)
            w_ready(3)

        @pl.when(t == 8)
        def _():
            w_other(4).wait_recv()
            w_fwd(4).start()

        @pl.when(t == 10)
        def _():
            w_ready(4)
            local(w, wo, loc.at[5]).start()

        @pl.when(t == 11)
        def _():
            x_send(1, RIGHT).wait_recv()
            x_relay(1, RIGHT).start()
            x_send(1, LEFT).wait_recv()
            x_relay(1, LEFT).start()

        @pl.when(t == 12)
        def _():
            finish_stats(0)

        @pl.when(t == 16)
        def _():
            x_relay(1, RIGHT).wait_recv()
            x_relay(1, LEFT).wait_recv()

        base = (t % TWO) * 2
        for u in BOTH:
            xcp(now[u], base + u).wait()

        for u in BOTH:
            r, j, k = place_of(now[u])

            @pl.when(j == 0)
            def _():
                cp = xt_out(r * nx + k, u)
                xtb[u] = xb[base + u].T
                cp.start()

        @pl.when((TWO * t + 2 < n_steps) & (t != 5))
        def _():
            for u in BOTH:
                xcp(later[u], 2 - base + u).start()

        @pl.when(t > 1)
        def _():
            for u in BOTH:
                zcp(older[u], base + u).wait()

        for u in BOTH:
            step(now[u], base + u)
        for u in BOTH:
            zcp(now[u], base + u).start()
            r, j, k = place_of(now[u])

            @pl.when(j == 0)
            def _():
                xt_out(r * nx + k, u).wait()

        return old, now, later

    none = (jnp.int32(0),) * TWO
    older, old, _ = lax.fori_loop(0, n_steps // TWO, body, (none, none, code_of(jnp.int32(0))))
    finish_stats(1)
    for u in BOTH:
        zcp(older[u], u).wait()
        zcp(old[u], TWO + u).wait()
    local(w, wo, loc.at[5]).wait()
    lab_own.wait()
    stat_own(0).wait()
    stat_own(1).wait()
    for r in BOTH:
        for right_way in (RIGHT, LEFT):
            x_send(r, right_way).wait_send()
            x_relay(r, right_way).wait_send()
    x_far.wait_send()
    for q in range(NCH):
        w_own(q).wait_send()
        w_other(q).wait_send()
        w_fwd(q).wait_send()
        w_core(q).wait_send()
    for i in range(len(peers)):
        lab_copy(i).wait_send()
        stat_copy(0, i).wait_send()
        stat_copy(1, i).wait_send()
    for sy in BOTH:
        for k in range(nx):
            def arrived():
                remote(lab_hbm, laba.at[sy, k], lsend.at[0], lrecv.at[sy, k], at.dev(c=at.pc)).wait_recv()
                for rr in BOTH:
                    remote(stm.at[rr], sta.at[sy, k, rr], ssend.at[0, 0], srecv.at[sy, k, rr], at.dev(c=at.pc)).wait_recv()

            if sy == 0:
                pl.when(k != x)(arrived)
            else:
                arrived()


def gather_logits(nx, ny, vocab, x, w, lab):
    tr, h = x.shape
    hk, vp = w.shape
    ch = vp // NCH
    shape = jax.ShapeDtypeStruct
    dma = pltpu.SemaphoreType.DMA
    vm = pltpu.VMEM
    flops = TWO * TWO * nx * tr * h * vp
    return pl.pallas_call(
        functools.partial(gather_logits_kernel, nx, ny, vocab),
        out_shape=(
            shape((TWO, nx, tr, h), BF16),
            shape((NCH, h, ch), BF16),
            shape((NCH, TWO, nx, tr, ch), F32),
            shape((TWO, nx, TWO, nx, SUB, tr), F32),
            shape((TWO, nx) + lab.shape, jnp.int32),
            shape((nx, h, TWO * tr), BF16),
        ),
        in_specs=[ANY] * 3,
        out_specs=(ANY,) * 6,
        scratch_shapes=[
            vm((NCH, h, ch), BF16), vm((tr, h), BF16),
            vm((4, tr, h), BF16), vm((4, tr, ch), F32), vm((NCH, SUB, TWO * LANES), F32),
            vm((TWO * nx, tr, LANES), F32), vm((TWO * nx, tr, LANES), F32), vm((TWO, nx, SUB, tr), F32), vm((TWO, h, tr), BF16),
            dma((TWO, 4)), dma((TWO, 4)), dma, dma, dma((3, NCH)), dma((3, NCH)), dma((NCH,)), dma((NCH,)),
            dma((TWO, TWO * nx - 1)), dma((TWO, nx, TWO)), dma((TWO * nx - 1,)), dma((TWO, nx)),
            dma((6,)), dma((NCH,)), dma((4,)), dma((4,)), dma((TWO,)),
        ],
        compiler_params=pltpu.CompilerParams(
            collective_id=0, has_side_effects=True, vmem_limit_bytes=60 * 2**20
        ),
        cost_estimate=pl.CostEstimate(flops=flops, bytes_accessed=4 * TWO * nx * tr * vp, transcendentals=0),
        name="gather_logits",
    )(x, w, lab)


def grads_kernel(
    nx, ny, inv, z, w_hbm, xt_hbm, st8, dxo, dwo, loss, rx, fx, dd, rr,
    w, xt, zb, gb, acc, dx, st, lacc, tmpa, tmpb, keep, fin, fdx, lbuf,
    wsem, tsem, zsem, xsend, xrecv, fsend, frecv, dsend, drecv, rsend, rrecv, osend, orecv, asem, bsem, lsend, lrecv,
    out_sem,
):
    at = Place(nx, ny)
    x, y, c = at.x, at.y, at.c
    tr, h = dxo.shape
    ch = zb.shape[2]
    sb = ch // TWO
    slot = NCH * sb
    hk = dwo.shape[0]
    nq = rx.shape[2]
    qr = tr // nq
    left, right = (x + nx - 1) % nx, (x + 1) % nx

    def par(yy, b):
        return jnp.where((yy + b) % TWO == 0, (yy + 1) % ny, (yy + ny - 1) % ny)

    def adj(yy, b):
        return jnp.where((yy + b) % TWO == 0, (yy + ny - 1) % ny, (yy + 1) % ny)

    for j in range(NCH):
        local(w_hbm.at[j], w.at[j], wsem.at[j]).start()
    barrier = pltpu.get_barrier_semaphore()
    for k in range(1, nx):
        pl.semaphore_signal(barrier, inc=1, device_id=at.dev(x=(x + k) % nx), device_id_type=MESH)
    for k in range(1, ny):
        pl.semaphore_signal(barrier, inc=1, device_id=at.dev(y=(y + k) % ny), device_id_type=MESH)
        pl.semaphore_signal(barrier, inc=1, device_id=at.dev(y=(y + k) % ny, c=at.pc), device_id_type=MESH)
    pl.semaphore_signal(barrier, inc=1, device_id=at.dev(c=at.pc), device_id_type=MESH)

    segments = ["x0", "w0", "w1", "x1", "w2", "w3", "x2", "w4", "x3"]
    segments += ["l%d" % j for j in range(NCH)]
    first, after, n_body = {}, {}, 0
    for seg in segments:
        first[seg] = n_body
        n_body += NCH if seg.startswith("x") else nx
        after[seg] = n_body

    def body_at(n):
        code, start = 0, 0
        for seg in segments[1:]:
            here = n >= first[seg]
            code = jnp.where(here, "xwl".index(seg[0]) * 8 + int(seg[-1]), code)
            start = jnp.where(here, first[seg], start)
        return code // 8, code % 8, n - start

    def tile(n, u):
        kind, i, k = body_at(n)
        mine = jnp.where(u == 0, (x + TWO * nx - 1 - i) % nx, (x + 1 + i) % nx)
        run = TWO * k + u
        is_x = kind == 0
        return jnp.where(is_x, k, i), jnp.where(is_x, u, run // nx), jnp.where(is_x, mine, run % nx)

    def zcp(n, u, buf):
        j, r, d = tile(n, u)
        return local(z.at[j, r, d], zb.at[buf], zsem.at[buf])

    for u in BOTH:
        zcp(0, u, u).start()
    local(xt_hbm, xt, tsem).start()

    def spread(run, _):
        st[run] = jnp.concatenate([st8[run // nx, run % nx]] * 16, axis=0).T
        return 0

    lax.fori_loop(0, TWO * nx, spread, 0)
    lacc[...] = jnp.zeros_like(lacc)
    pl.semaphore_wait(barrier, nx - 1 + TWO * (ny - 1) + 1)

    def x_copy(s, dr, q):
        return remote(
            dx.at[s % TWO, dr, pl.ds(pl.multiple_of(q * qr, SUB), qr)], rx.at[s, dr, q],
            xsend.at[s, dr, q], xrecv.at[s, dr, q], at.dev(x=left if dr else right),
        )

    def far_copy(q):
        return remote(
            dx.at[1, 1, pl.ds(pl.multiple_of(q * qr, SUB), qr)], fx.at[q], fsend.at[q], frecv.at[q], at.dev(y=at.far)
        )

    def a_load(s, q, dr):
        return local(rx.at[s - 1, dr, q], tmpa.at[q % TWO, dr], asem.at[q % TWO, dr])

    def a_pre(s, q):
        for dr in BOTH:
            x_copy(s - 1, dr, q).wait_recv()
            a_load(s, q, dr).start()

    def a_use(s, q):
        rows = pl.ds(pl.multiple_of(q * qr, SUB), qr)
        for dr in BOTH:
            a_load(s, q, dr).wait()
            dx[s % TWO, dr, rows, :] += tmpa[q % TWO, dr]

        @pl.when(s < nx - 1)
        def _():
            for dr in BOTH:
                x_copy(s, dr, q).start()

        @pl.when(s == nx - 1)
        def _():
            far_copy(q).start()

    def f_load(q):
        return local(fx.at[q], tmpa.at[q % TWO, 0], asem.at[q % TWO, 0])

    def f_out(q):
        return local(fdx.at[q % TWO], dxo.at[pl.ds(pl.multiple_of(q * qr, 16), qr)], out_sem.at[q])

    def f_pre(q):
        far_copy(q).wait_recv()
        f_load(q).start()

    def f_use(q):
        f_load(q).wait()

        @pl.when(q > 1)
        def _():
            f_out(q - 2).wait()

        rows = pl.ds(pl.multiple_of(q * qr, SUB), qr)
        fdx[q % TWO] = (dx[1, 0, rows] + tmpa[q % TWO, 0]).astype(BF16)
        f_out(q).start()

    def lot(b):
        q = (c + b) % TWO
        slices = [(b + TWO * q) % ny, (b + 1 + TWO * q) % ny]
        other = [(b + TWO * (1 - q)) % ny, (b + 1 + TWO * (1 - q)) % ny]
        home = half_of(y, b, ny) == q
        kt = jnp.where(home, y, adj(y, b))
        it = jnp.where(slices[0] == kt, 0, 1)
        return slices, other, kt, it, home

    def rows_of(k):
        return pl.ds(pl.multiple_of(k * hk, 16), hk)

    def d_copy(j, b, i):
        other = lot(b)[1]
        return remote(
            acc.at[j % TWO, rows_of(other[i]), pl.ds(b * sb, sb)], dd.at[j, b, i],
            dsend.at[j, b, i], drecv.at[j, b, i], at.dev(c=at.pc),
        )

    def d_send(j):
        for b in BOTH:
            for i in BOTH:
                d_copy(j, b, i).start()

    def r_load(j, b, i):
        return local(dd.at[j, b, i], tmpb.at[b, i], bsem.at[b, i])

    def r_pre(j):
        for b in BOTH:
            for i in BOTH:
                d_copy(j, b, i).wait_recv()
                r_load(j, b, i).start()

    def r_copy(j, b):
        slices, _, _, it, _ = lot(b)
        kg = jnp.where(it == 0, slices[1], slices[0])
        src = acc.at[j % TWO, rows_of(kg), pl.ds(b * sb, sb)]
        return remote(src, rr.at[j, b], rsend.at[j, b], rrecv.at[j, b], at.dev(y=par(y, b)))

    def r_use(j):
        for b in BOTH:
            slices, _, kt, it, _ = lot(b)
            kg = jnp.where(it == 0, slices[1], slices[0])
            for i in BOTH:
                r_load(j, b, i).wait()

            acc[j % TWO, rows_of(kg), pl.ds(b * sb, sb)] += tmpb[b, 1 - it]
            r_copy(j, b).start()
            keep[j % TWO, b] = acc[j % TWO, rows_of(kt), pl.ds(b * sb, sb)] + tmpb[b, it]

    def s_load(j, b):
        return local(rr.at[j, b], tmpb.at[b, 0], bsem.at[b, 0])

    def s_pre(j):
        for b in BOTH:
            r_copy(j, b).wait_recv()
            s_load(j, b).start()

    def o_copy(j, b):
        kt = lot(b)[2]
        f = half_of(y, b, ny)
        dst = dwo.at[:, pl.ds(pl.multiple_of(f * slot + j * sb, LANES), sb)]
        return remote(fin.at[b], dst, osend.at[j, b], orecv.at[f, j], at.dev(y=kt, c=b))

    def o_here(j, b):
        f = half_of(y, b, ny)
        dst = dwo.at[:, pl.ds(pl.multiple_of(f * slot + j * sb, LANES), sb)]
        return local(fin.at[b], dst, orecv.at[f, j])

    def is_here(b):
        return lot(b)[4] & (c == b)

    def s_use(j):
        for b in BOTH:
            s_load(j, b).wait()

            @pl.when((j > 0) & jnp.logical_not(is_here(b)))
            def _():
                o_copy(j - 1, b).wait_send()

            @pl.when((j > 0) & is_here(b))
            def _():
                o_here(j - 1, b).wait()

            fin[b] = (keep[j % TWO, b] + tmpb[b, 0]).astype(BF16)

            @pl.when(is_here(b))
            def _():
                o_here(j, b).start()

            @pl.when(jnp.logical_not(is_here(b)))
            def _():
                o_copy(j, b).start()

    def l_copy(stage, k):
        if stage == 0:
            return remote(lbuf.at[0, x], lbuf.at[0, x], lsend.at[0, k], lrecv.at[0, x], at.dev(x=(x + k) % nx))
        if stage == 1:
            return remote(lbuf.at[1, y], lbuf.at[1, y], lsend.at[1, k], lrecv.at[1, y], at.dev(y=(y + k) % ny))
        return remote(lbuf.at[2, c], lbuf.at[2, c], lsend.at[2, 0], lrecv.at[2, c], at.dev(c=at.pc))

    def l_sum(stage, size, me):
        for k in range(size):
            @pl.when(k != me)
            def _():
                remote(
                    lbuf.at[stage, k], lbuf.at[stage, k], lsend.at[stage, 0], lrecv.at[stage, k], at.dev(c=at.pc)
                ).wait_recv()

        total = lbuf[stage, 0]
        for k in range(1, size):
            total = total + lbuf[stage, k]
        return total

    def l_start():
        lbuf[0, x] = -lacc[...]
        for k in range(1, nx):
            l_copy(0, k).start()

    def l_mid():
        lbuf[1, y] = l_sum(0, nx, x)
        for k in range(1, ny):
            l_copy(1, k).start()

    def l_late():
        lbuf[2, c] = l_sum(1, ny, y)
        l_copy(2, 0).start()

    lane = lax.broadcasted_iota(jnp.int32, (min(64, tr), LANES), 1).astype(F32)

    def each_tile(n, u, buf, c0, c1, fn):
        j, r, d = tile(n, u)
        blk = min(64, tr)
        for o in range(0, tr, blk):
            rows = slice(o, o + blk)
            t = st[r * nx + d, rows, :]
            shift = jnp.broadcast_to(t[:, 0:1], (blk, LANES))
            lab = jnp.broadcast_to(t[:, 1:TWO], (blk, LANES)) - (j * ch).astype(F32)
            for e in range(c0 // LANES, c1 // LANES):
                cols = slice(LANES * e, LANES * e + LANES)
                fn(rows, cols, zb[buf, rows, cols] - shift, lane + float(LANES * e) == lab)

    def make_g(n, u, buf, c0, c1):
        def one(rows, cols, dist, hit):
            g = jnp.exp(dist)
            gb[u, rows, cols] = jnp.where(hit, g - inv, g).astype(BF16)

        each_tile(n, u, buf, c0, c1, one)

    def l_body(n, base):
        total = [jnp.zeros((SUB, LANES), F32)]

        def one(rows, cols, dist, hit):
            total[0] = total[0] + jnp.sum(jnp.where(hit, dist, 0.0).reshape(-1, SUB, LANES), axis=0)

        for u in BOTH:
            each_tile(n, u, base + u, 0, ch, one)
        lacc[...] += total[0]

    big = ch % (10 * LANES) == 0
    x_cuts = [(ch * e // 5, ch * (e + 1) // 5) for e in range(5)] if big else [(0, ch)]
    w_cuts = [(0, ch // 5), (ch // 5, ch * 3 // 5), (ch * 3 // 5, ch)] if big else [(0, ch)]

    def x_body(n, base):
        _, s, j = body_at(n)
        half = s % TWO

        @pl.when(j == 0)
        def _():
            dx[half] = jnp.zeros(dx.shape[1:], F32)

        for u in BOTH:
            for c0, c1 in x_cuts:
                make_g(n, u, base + u, c0, c1)
                dx[half, u] += lax.dot_general(
                    gb[u, :, c0:c1], w[j, :, c0:c1], (((1,), (1,)), ((), ())), preferred_element_type=F32
                )

    def w_body(n, base):
        _, j, k = body_at(n)
        half = j % TWO

        @pl.when(k == 0)
        def _():
            acc[half] = jnp.zeros(acc.shape[1:], F32)

        for c0, c1 in w_cuts:
            for u in BOTH:
                make_g(n, u, base + u, c0, c1)
            acc[half, :, c0:c1] += jnp.dot(
                xt[k], gb[:, :, c0:c1].reshape(TWO * tr, c1 - c0), preferred_element_type=F32
            )

    late = after["x3"]
    plan_a = [(after["x1"] + q, 1, q) for q in range(nq)] + [(after["x2"] + q, 2, q) for q in range(nq)]
    plan_a += [(late + 1 + 7 * q - q // 3 * 2, 3, q) for q in range(nq)]
    plan_r = [(11, 12, 0), (15, 17, 1), (24, 25, 2), (28, 30, 3), (37, 38, 4)]
    plan_s = [(18, 19, 0), (22, 23, 1), (31, 32, 2), (35, 36, 3), (late + 6, late + 7, 4)]
    pre_r, use_r = [(p, j) for p, _, j in plan_r], [(u, j) for _, u, j in plan_r]
    pre_s, use_s = [(p, j) for p, _, j in plan_s], [(u, j) for _, u, j in plan_s]
    plan_f = [(late + 11, 0), (late + 18, 1), (n_body + TWO, 2), (n_body + 4, 3)]
    n_all = n_body + 5

    def when(n, table, fn):
        table = [(e[0], e[1:]) for e in table]
        hit = functools.reduce(lambda p, q: p | q, [n == e for e, _ in table])

        @pl.when(hit)
        def _():
            args = []
            for i in range(len(table[0][1])):
                val = 0
                for e, vals in table:
                    if vals[i]:
                        val = val + jnp.where(n == e, vals[i], 0)
                args.append(val + jnp.int32(0))
            fn(*args)

    def body(n, _):
        @pl.when(n < NCH)
        def _():
            local(w_hbm.at[n], w.at[n], wsem.at[n]).wait()

        @pl.when(n == first["w0"])
        def _():
            local(xt_hbm, xt, tsem).wait()
            for q in range(nq):
                for dr in BOTH:
                    x_copy(0, dr, q).start()

        when(n, [(after["w%d" % j], j) for j in range(NCH)], d_send)
        when(n, plan_a, a_use)
        when(n, plan_f, f_use)
        when(n, use_r, r_use)
        when(n, use_s, s_use)
        when(n, [(e[0] - 1,) + e[1:] for e in plan_a], a_pre)
        when(n, [(e[0] - 1,) + e[1:] for e in plan_f], f_pre)
        when(n, pre_r, r_pre)
        when(n, pre_s, s_pre)

        for at_n, fn in ((n_body, l_start), (n_body + TWO, l_mid), (n_body + 4, l_late)):
            pl.when(n == at_n)(fn)

        @pl.when((n == first["x2"]) | (n == first["x3"]))
        def _():
            s = jnp.where(n == first["x2"], 0, 1)
            for q in range(nq):
                for dr in BOTH:
                    x_copy(s, dr, q).wait_send()

        for j in range(2, NCH):
            @pl.when(n == first["w%d" % j])
            def _():
                for b in BOTH:
                    r_copy(j - 2, b).wait_send()
                    for i in BOTH:
                        d_copy(j - 2, b, i).wait_send()

        base = (n % TWO) * 2

        @pl.when(n < n_body)
        def _():
            for u in BOTH:
                zcp(n, u, base + u).wait()

            @pl.when(n + 1 < n_body)
            def _():
                for u in BOTH:
                    zcp(n + 1, u, 2 - base + u).start()

            kind = body_at(n)[0]

            @pl.when(kind == 0)
            def _():
                x_body(n, base)

            @pl.when(kind == 1)
            def _():
                w_body(n, base)

            @pl.when(kind == TWO)
            def _():
                l_body(n, base)

        return 0

    lax.fori_loop(0, n_all, body, 0)
    loss[...] = l_sum(2, TWO, c)

    for q in range(nq):
        if q >= nq - 2:
            f_out(q).wait()
        far_copy(q).wait_send()
        for dr in BOTH:
            x_copy(2, dr, q).wait_send()
    for b in BOTH:
        for j in range(NCH - 2, NCH):
            for i in BOTH:
                d_copy(j, b, i).wait_send()
            r_copy(j, b).wait_send()

        @pl.when(is_here(b))
        def _():
            o_here(NCH - 1, b).wait()

        @pl.when(jnp.logical_not(is_here(b)))
        def _():
            o_copy(NCH - 1, b).wait_send()

    q0 = half_of(y, c, ny)
    for f in BOTH:
        kept = (f == q0) & ((q0 + c) % TWO == c)

        @pl.when(jnp.logical_not(kept))
        def _():
            for j in range(NCH):
                dst = dwo.at[:, pl.ds(f * slot + j * sb, sb)]
                remote(fin.at[0], dst, osend.at[j, 0], orecv.at[f, j], at.dev(c=at.pc)).wait_recv()

    for k in range(1, nx):
        l_copy(0, k).wait_send()
    for k in range(1, ny):
        l_copy(1, k).wait_send()
    l_copy(2, 0).wait_send()


def grads(nx, ny, inv, z, w, xt, st8, hk):
    h = w.shape[1]
    ch = w.shape[2]
    tr = z.shape[3]
    nq = 4
    shape = jax.ShapeDtypeStruct
    dma = pltpu.SemaphoreType.DMA
    vm = pltpu.VMEM
    vspec = pl.BlockSpec(memory_space=pltpu.VMEM)
    sb, qr = ch // TWO, tr // nq
    return pl.pallas_call(
        functools.partial(grads_kernel, nx, ny, inv),
        out_shape=(
            shape((tr, h), BF16), shape((hk, NCH * ch), BF16), shape((SUB, LANES), F32),
            shape((nx - 1, TWO, nq, qr, h), F32), shape((nq, qr, h), F32),
            shape((NCH, TWO, TWO, hk, sb), F32), shape((NCH, TWO, hk, sb), F32),
        ),
        in_specs=[ANY, ANY, ANY, vspec],
        out_specs=(ANY, ANY, vspec, ANY, ANY, ANY, ANY),
        scratch_shapes=[
            vm((NCH, h, ch), BF16), vm((nx, h, TWO * tr), BF16), vm((4, tr, ch), F32), vm((TWO, tr, ch), BF16),
            vm((TWO, h, ch), F32), vm((TWO, TWO, tr, h), F32), vm((TWO * nx, tr, LANES), F32), vm((SUB, LANES), F32),
            vm((TWO, TWO, qr, h), F32), vm((TWO, TWO, hk, sb), F32), vm((TWO, TWO, hk, sb), F32),
            vm((TWO, hk, sb), BF16), vm((TWO, qr, h), BF16), vm((3, max(nx, ny), SUB, LANES), F32),
            dma((NCH,)), dma, dma((4,)), dma((nx - 1, TWO, nq)), dma((nx - 1, TWO, nq)), dma((nq,)), dma((nq,)),
            dma((NCH, TWO, TWO)), dma((NCH, TWO, TWO)), dma((NCH, TWO)), dma((NCH, TWO)), dma((NCH, TWO)), dma((TWO, NCH)),
            dma((TWO, TWO)), dma((TWO, TWO)), dma((3, max(nx, ny))), dma((3, max(nx, ny))), dma((nq,)),
        ],
        compiler_params=pltpu.CompilerParams(
            collective_id=1, has_side_effects=True, vmem_limit_bytes=67_000_000
        ),
        name="grads",
    )(z, w, xt, st8)


def solution(mesh):
    ny = mesh.shape["fsdp"]
    tp_size = mesh.shape["tp"]
    nx = tp_size // TWO
    token_spec = P(("dp", "fsdp", "tp"), None)
    label_spec = P(("dp", "fsdp", "tp"))

    def local_step(hidden, w_head, labels):
        tr, h = hidden.shape
        hk, vocab = w_head.shape
        inv = 1.0 / (tr * tp_size * ny)
        vp = -(-vocab // (256 * NCH)) * (256 * NCH)
        ch = vp // NCH
        sb = ch // TWO
        slot = NCH * sb
        tp = lax.axis_index("tp")
        x, y = tp // TWO, lax.axis_index("fsdp")
        w_pad = jnp.pad(w_head, ((0, 0), (0, vp - vocab)))
        lab8 = jnp.pad(labels.reshape(-1, LANES), ((0, SUB - tr // LANES), (0, 0)))
        xg, wg, z, sta, laba, xt = gather_logits(nx, ny, vocab, hidden, w_pad, lab8)

        ms = sta[..., 0, :].reshape(TWO * nx, TWO, nx, tr)
        ss = sta[..., 1, :].reshape(TWO * nx, TWO, nx, tr)
        top = jnp.max(ms, axis=0)
        tot = jnp.sum(ss * jnp.exp(ms - top), axis=0)
        lab = laba[:, :, 0 : tr // LANES, :].reshape(2, nx, tr)
        shard, off = lab // vocab, lab % vocab
        b, f = shard % TWO, off // slot
        pos = off - f * slot
        mine = (shard // TWO == x) & (half_of(y, b, ny) == f)
        col = jnp.where(mine, (pos // sb) * ch + b * sb + pos % sb, -1)
        rows = [top + jnp.log(tot) - jnp.log(inv), col.astype(F32)]
        st8 = jnp.stack(rows + [jnp.zeros_like(top)] * 6, axis=2)
        d_hidden, d_w, loss = grads(nx, ny, inv, z, wg, xt, st8, hk)[:3]
        mean_loss = jnp.sum(loss) * inv + jnp.log(inv)
        return mean_loss.reshape(1), d_hidden, d_w[:, :vocab]

    return jax.shard_map(
        local_step,
        mesh=mesh,
        in_specs=(token_spec, P("fsdp", "tp"), label_spec),
        out_specs=(P("dp"), token_spec, P(("dp", "fsdp"), "tp")),
        check_vma=False,
    )
```

time: 451 us -> 409 us (0.907)
  the two profiles are of different devices: /device:TPU:111 before, /device:TPU:97 now
where the time goes in v3:
time: 409 us; the launch traced here: 408 us
  Pallas kernels  384 us (94%)
  local copies, waits for them, and re-layouts  13.9 us (3%)
  other arithmetic  7.46 us (2%)
    pallas_call x1, Pallas kernels, grads(): pl.pallas_call(functools.partial(grads_kernel, nx, ny, inv), out_shape=(s...  223 us
    pallas_call x1, Pallas kernels, gather_logits(): pl.pallas_call(functools.partial(gather_logits_kernel, nx, ny, vocab), ou...  161 us
    unnamed x5, local copies, waits for them, and re-layouts  10.6 us

profile of v3, /device:TPU:97, one launch (start us, length us, event | category | flops | bytes accessed | tf_op | source)
XLA Modules:
  0.0 407.6 jit_solution(11957075548699123514)
XLA Ops:
  0.7 0.1 pad.13.clone
  0.7 0.1 pad.12.clone
  0.8 1.3 pad.9.lab_hbm
  2.1 4.0 copy.8
  6.1 1.9 pad.8.w_hbm
  8.0 160.7 %gather_logits.1 = (bf16[2,4,512,1024]{3,2,1,0:T(8,128)(2,1)}, bf16[5,1024,1280]{2,1,0:T(8,128)(2,1)}, f32[5,2,4,512,1280]{4,3,2,1,0:T(8,128)}, f32[2,4,2,4,8,51...) custom-call(bf16[512,1024]{1,0:T(8,128)(2,1)} %x_hbm.1, bf16[256,6400]{1,0:T(8,128)(2,1)} %pad.8.w_hbm, ...), custom_call_target="tpu_custom_call" | custom-call | flops 53687091200 | bytes 104857600 | tf_op jit(solution)/shard_map/gather_logits/pallas_call | solution.py:417
  168.7 0.8 sign_compare_fusion
  169.5 0.8 slice_divide_fusion
  170.3 0.6 fusion.2
  170.8 1.4 slice_reduce_fusion
  172.2 1.9 multiply_reduce_fusion
  174.1 0.7 maximum_maximum_fusion.st8
  174.8 223.0 %grads.1 = (bf16[512,1024]{1,0:T(8,128)(2,1)}, bf16[256,6400]{1,0:T(8,128)(2,1)}, f32[8,128]{1,0:T(8,128)}, f32[3,2,4,128,1024]{4,3,2,1,0:T(8,128)}, f32[4,128,1...) custom-call(f32[5,2,4,512,1280]{4,3,2,1,0:T(8,128)} %get-tuple-element.11.z, ...), custom_call_target="tpu_custom_call" | custom-call | tf_op jit(solution)/shard_map/grads/pallas_call | solution.py:908
  397.9 0.0 copy-start
  397.9 1.4 reduce_sum.19
  399.9 5.6 %copy.10 = bf16[256,6288]{0,1:T(8,128)(2,1)} copy(bf16[256,6288]{1,0:T(8,128)(2,1)} %bitcast.5) | data formatting | bytes 6438912
  405.5 0.0 copy-done
  405.5 1.0 copy.12
  (5 shorter events, 0.0 us)
Async XLA Ops:
  397.9 7.6 %copy-start = (bf16[512,1024]{1,0:T(8,128)(2,1)S(1)}, bf16[512,1024]{1,0:T(8,128)(2,1)}, u32[]{:S(2)}) copy-start(bf16[512,1024]{1,0:T(8,128)(2,1)} %get-tuple-element.31) | copy-start | bytes 3145732

commit v4 on v3

--- a/solution.py
+++ b/solution.py
@@ -1,4 +1,5 @@
 import functools
+import math
 
 import jax
 import jax.numpy as jnp
@@ -66,17 +67,30 @@
 def gather_logits_kernel(
     nx, ny, vocab,
     x_hbm, w_hbm, lab_hbm, xg, wo, z, sta, laba, xt,
-    w, xown, xb, zb, bias, m, s, stm, xtb,
-    xsend, xrecv, ysend, yrecv, wsend, wrecv, dsend, drecv, ssend, srecv, lsend, lrecv, loc, wloc, xsem, zsem, tsem,
+    w, wsrc, xown, xb, zb, bias, m, s, stm, xtb,
+    xsend, xrecv, ysend, yrecv, wsend, wrecv, dsend, drecv, ssend, srecv, lsend, lrecv, loc, wloc, xsem, zsem, tsem, wload,
 ):
     at = Place(nx, ny)
     x, y, c = at.x, at.y, at.c
     tr = xown.shape[0]
-    hk = w_hbm.shape[0]
-    sb = w.shape[2] // TWO
+    hk = w_hbm.shape[1]
+    sb = w.shape[1] // TWO
     slot = NCH * sb
     left, right = (x + nx - 1) % nx, (x + 1) % nx
     top, bot = pl.ds(0, tr // TWO), pl.ds(tr // TWO, tr // TWO)
+
+    def rows_in(f, q):
+        return min(sb, vocab - f * slot - q * sb)
+
+    def w_load(f, q):
+        n = rows_in(f, q)
+        src = w_hbm.at[pl.ds(f * slot + q * sb, n)]
+        return local(src, wsrc.at[f * NCH + q, pl.ds(0, n)], wload.at[f * NCH + q])
+
+    def preload():
+        for q in range(NCH):
+            for f in BOTH:
+                w_load(f, q).start()
 
     barrier = pltpu.get_barrier_semaphore()
     for k in range(1, nx):
@@ -88,6 +102,7 @@
     pl.semaphore_signal(barrier, inc=1, device_id=at.dev(c=at.pc), device_id_type=MESH)
     load_x = local(x_hbm, xown, loc.at[0])
     load_x.start()
+    preload()
     pl.semaphore_wait(barrier, TWO * nx + 2)
     load_x.wait()
 
@@ -106,11 +121,13 @@
     x_far = remote(xown, xg.at[1, x], ysend, yrecv, at.dev(y=at.far))
     keep_x = local(xown, xg.at[0, x], loc.at[1])
 
+    blocks = [(f, q) for f in BOTH for q in range(NCH)]
+
     def w_src(f, q):
-        return w_hbm.at[:, pl.ds(pl.multiple_of(f * slot + q * sb, LANES), sb)]
+        return wsrc.at[f * NCH + q]
 
     def w_dst(k, q):
-        return w.at[q, pl.ds(pl.multiple_of(k * hk, 16), hk), pl.ds(pl.multiple_of(c * sb, LANES), sb)]
+        return w.at[q, pl.ds(pl.multiple_of(c * sb, SUB), sb), pl.ds(pl.multiple_of(k * hk, LANES), hk)]
 
     def w_own(q):
         return remote(w_src(at.half, q), w_dst(y, q), wsend.at[0, q], wrecv.at[0, q], at.dev(y=at.p))
@@ -118,26 +135,43 @@
     def w_other(q):
         return remote(w_src(1 - at.half, q), w_dst(y, q), wsend.at[1, q], wrecv.at[1, q], at.dev(y=at.a))
 
-    def w_fwd(q):
-        return remote(w_dst(at.a, q), w_dst(at.a, q), wsend.at[2, q], wrecv.at[2, q], at.dev(y=at.p))
+    def w_far(q):
+        return remote(w_src(1 - at.half, q), w_dst(y, q), wsend.at[2, q], wrecv.at[2, q], at.dev(y=at.far))
 
     def w_core(q):
-        part = w.at[q, :, pl.ds(pl.multiple_of(c * sb, LANES), sb)]
+        part = w.at[q, pl.ds(pl.multiple_of(c * sb, SUB), sb)]
         return remote(part, part, dsend.at[q], drecv.at[q], at.dev(c=at.pc))
 
-    def w_local(q):
-        return local(w_src(at.half, q), w_dst(y, q), wloc.at[q])
+    def w_local(f, q):
+        n = rows_in(f, q)
+        dst = w.at[q, pl.ds(pl.multiple_of(c * sb, SUB), n), pl.ds(pl.multiple_of(y * hk, LANES), hk)]
+        return local(w_hbm.at[pl.ds(f * slot + q * sb, n)], dst, wloc.at[q])
 
     def w_out(q):
         w_own(q).start()
         w_other(q).start()
-
-    w_out(0)
+        w_far(q).start()
+
     x_send(0, RIGHT).start()
     x_send(0, LEFT).start()
+    for q in range(NCH):
+        for f in BOTH:
+            w_load(f, q).wait()
+            if rows_in(f, q) < sb:
+                pad = sb - rows_in(f, q)
+                wsrc[f * NCH + q, sb - pad :, :] = jnp.zeros((pad, hk), BF16)
+        w_out(q)
+        if q == 0:
+            x_far.start()
     keep_x.start()
-    for q in range(NCH):
-        w_local(q).start()
+    for f, q in blocks:
+        @pl.when(at.half == f)
+        def _():
+            w_local(f, q).start()
+            if rows_in(f, q) < sb:
+                pad = sb - rows_in(f, q)
+                at_row = pl.multiple_of(c * sb + sb - pad, SUB)
+                w[q, pl.ds(at_row, pad), pl.ds(pl.multiple_of(y * hk, LANES), hk)] = jnp.zeros((pad, hk), BF16)
 
     peers = [(0, k) for k in range(1, nx)] + [(1, k) for k in range(nx)]
 
@@ -167,12 +201,6 @@
             xtb.at[u], xt.at[run // TWO, :, pl.ds(pl.multiple_of((run % TWO) * tr, LANES), tr)], tsem.at[u]
         )
 
-    w_other(0).wait_recv()
-    w_fwd(0).start()
-    w_out(1)
-    w_other(1).wait_recv()
-    w_fwd(1).start()
-    w_out(2)
     keep_x.wait()
     x_send(0, RIGHT).wait_recv()
     x_relay(0, RIGHT).start()
@@ -181,14 +209,12 @@
 
     n_steps = TWO * nx * NCH
 
-    order = [(0, k, j) for k in (0, 3, 1, TWO) for j in BOTH]
-    order += [(0, k, TWO) for k in (0, 3, 1, TWO)]
-    order += [(1, 0, 0), (1, 0, 1)]
-    order += [(0, k, 3) for k in (0, 3, 1, TWO)]
-    order += [(1, 0, TWO), (1, 0, 3)]
-    order += [(0, k, 4) for k in (0, 3, 1, TWO)]
-    order += [(1, 0, 4)] + [(1, k, j) for k in (3, 1, TWO) for j in range(NCH)]
-
+    near = (0, 3, 1, 2)
+    order = [(0, k, 0) for k in near] + [(1, 0, 0)]
+    order += [(0, k, 1) for k in near] + [(1, 0, 1)]
+    order += [(1, k, j) for j in BOTH for k in (3, 1)]
+    order += [(0, k, 2) for k in near] + [(1, k, 2) for k in (0, 3, 1)] + [(1, 2, j) for j in range(3)]
+    order += [(r, k, j) for j in (3, 4) for r in BOTH for k in near]
     codes = [(r * 4 + k) * 8 + j for r, k, j in order]
 
     def code_of(t):
@@ -212,7 +238,7 @@
         c0 = 0
         for width in (sb * 4 // 5, TWO * sb - sb * 4 // 5) if sb % 640 == 0 else (2 * sb,):
             cols = slice(c0, c0 + width)
-            zz = jnp.dot(xb[u], w[j, :, cols], preferred_element_type=F32)
+            zz = lax.dot_general(xb[u], w[j, cols, :], (((1,), (1,)), ((), ())), preferred_element_type=F32)
             zb[u, :, cols] = zz
             blk = min(64, tr)
             for o in range(0, tr, blk):
@@ -247,27 +273,29 @@
         return local(stm.at[r], sta.at[0, x, r], loc.at[3 + r])
 
     def finish_stats(r):
-        def one(d, _):
-            run = r * nx + d
-            mm = m[run]
+        lane = lax.broadcasted_iota(jnp.int32, m.shape[1:], 1)
+        blk = jnp.zeros(m.shape[1:], F32)
+        for d in range(nx):
+            mm = m[r * nx + d]
             top_m = jnp.max(mm, axis=1, keepdims=True)
-            tot = jnp.sum(s[run] * jnp.exp(mm - top_m), axis=1, keepdims=True)
-            lane = lax.broadcasted_iota(jnp.int32, mm.shape, 1)
-            blk = jnp.where(lane == 0, top_m, jnp.where(lane == 1, tot, 0.0))
-            stm[r, d] = blk.T[0:SUB, :]
-            return 0
-
-        lax.fori_loop(0, nx, one, 0)
+            tot = jnp.sum(s[r * nx + d] * jnp.exp(mm - top_m), axis=1, keepdims=True)
+            blk = jnp.where(lane == d, top_m, jnp.where(lane == nx + d, tot, blk))
+        stm[r] = blk.T[0:SUB, :]
         for i in range(len(peers)):
             stat_copy(r, i).start()
         stat_own(r).start()
 
-    def w_ready(j):
-        w_local(j).wait()
+    def w_here(j):
+        for f in BOTH:
+            pl.when(at.half == f)(w_local(f, j).wait)
+
         w_own(j).wait_recv()
-        w_fwd(j).wait_recv()
+        w_other(j).wait_recv()
+        w_far(j).wait_recv()
         w_core(j).start()
-        w_core(j).wait_recv()
+
+    here_at = (0, 2, 6, 11, 15)
+    both_at = (0, 2, 7, 12, 16)
 
     def body(t, held):
         older, old, now = held
@@ -277,62 +305,38 @@
         def _():
             for u in BOTH:
                 xcp(now[u], u).start()
-            w_ready(0)
-            w_ready(1)
-
-        @pl.when(t == 2)
-        def _():
-            w_other(2).wait_recv()
-            w_fwd(2).start()
-            x_far.start()
-            w_out(3)
             x_relay(0, RIGHT).wait_recv()
             x_relay(0, LEFT).wait_recv()
 
-        @pl.when(t == 4)
-        def _():
-            w_ready(2)
-
-        @pl.when(t == 6)
+        for j in range(NCH):
+            pl.when(t == here_at[j])(functools.partial(w_here, j))
+            pl.when(t == both_at[j])(w_core(j).wait_recv)
+
+        @pl.when(t == 1)
         def _():
             x_far.wait_recv()
             x_send(1, RIGHT).start()
             x_send(1, LEFT).start()
-            for u in BOTH:
-                xcp(now[u], u).start()
-
-        @pl.when(t == 7)
-        def _():
-            w_other(3).wait_recv()
-            w_fwd(3).start()
-            w_out(4)
-            w_ready(3)
-
-        @pl.when(t == 8)
-        def _():
-            w_other(4).wait_recv()
-            w_fwd(4).start()
-
-        @pl.when(t == 10)
-        def _():
-            w_ready(4)
-            local(w, wo, loc.at[5]).start()
-
-        @pl.when(t == 11)
+
+        @pl.when(t == 4)
         def _():
             x_send(1, RIGHT).wait_recv()
             x_relay(1, RIGHT).start()
             x_send(1, LEFT).wait_recv()
             x_relay(1, LEFT).start()
 
-        @pl.when(t == 12)
-        def _():
-            finish_stats(0)
-
-        @pl.when(t == 16)
+        @pl.when(t == 9)
         def _():
             x_relay(1, RIGHT).wait_recv()
             x_relay(1, LEFT).wait_recv()
+
+        @pl.when(t == 16)
+        def _():
+            local(w, wo, loc.at[5]).start()
+
+        @pl.when(t == 18)
+        def _():
+            finish_stats(0)
 
         base = (t % TWO) * 2
         for u in BOTH:
@@ -347,7 +351,7 @@
                 xtb[u] = xb[base + u].T
                 cp.start()
 
-        @pl.when((TWO * t + 2 < n_steps) & (t != 5))
+        @pl.when(TWO * t + 2 < n_steps)
         def _():
             for u in BOTH:
                 xcp(later[u], 2 - base + u).start()
@@ -387,7 +391,7 @@
     for q in range(NCH):
         w_own(q).wait_send()
         w_other(q).wait_send()
-        w_fwd(q).wait_send()
+        w_far(q).wait_send()
         w_core(q).wait_send()
     for i in range(len(peers)):
         lab_copy(i).wait_send()
@@ -408,7 +412,8 @@
 
 def gather_logits(nx, ny, vocab, x, w, lab):
     tr, h = x.shape
-    hk, vp = w.shape
+    hk = w.shape[1]
+    vp = -(-vocab // (TWO * LANES * NCH)) * TWO * LANES * NCH
     ch = vp // NCH
     shape = jax.ShapeDtypeStruct
     dma = pltpu.SemaphoreType.DMA
@@ -418,21 +423,21 @@
         functools.partial(gather_logits_kernel, nx, ny, vocab),
         out_shape=(
             shape((TWO, nx, tr, h), BF16),
-            shape((NCH, h, ch), BF16),
+            shape((NCH, ch, h), BF16),
             shape((NCH, TWO, nx, tr, ch), F32),
-            shape((TWO, nx, TWO, nx, SUB, tr), F32),
+            shape((TWO, nx, TWO, SUB, tr), F32),
             shape((TWO, nx) + lab.shape, jnp.int32),
             shape((nx, h, TWO * tr), BF16),
         ),
         in_specs=[ANY] * 3,
         out_specs=(ANY,) * 6,
         scratch_shapes=[
-            vm((NCH, h, ch), BF16), vm((tr, h), BF16),
+            vm((NCH, ch, h), BF16), vm((TWO * NCH, ch // TWO, hk), BF16), vm((tr, h), BF16),
             vm((4, tr, h), BF16), vm((4, tr, ch), F32), vm((NCH, SUB, TWO * LANES), F32),
-            vm((TWO * nx, tr, LANES), F32), vm((TWO * nx, tr, LANES), F32), vm((TWO, nx, SUB, tr), F32), vm((TWO, h, tr), BF16),
+            vm((TWO * nx, tr, LANES), F32), vm((TWO * nx, tr, LANES), F32), vm((TWO, SUB, tr), F32), vm((TWO, h, tr), BF16),
             dma((TWO, 4)), dma((TWO, 4)), dma, dma, dma((3, NCH)), dma((3, NCH)), dma((NCH,)), dma((NCH,)),
             dma((TWO, TWO * nx - 1)), dma((TWO, nx, TWO)), dma((TWO * nx - 1,)), dma((TWO, nx)),
-            dma((6,)), dma((NCH,)), dma((4,)), dma((4,)), dma((TWO,)),
+            dma((6,)), dma((NCH,)), dma((4,)), dma((4,)), dma((TWO,)), dma((TWO * NCH,)),
         ],
         compiler_params=pltpu.CompilerParams(
             collective_id=0, has_side_effects=True, vmem_limit_bytes=60 * 2**20
@@ -443,10 +448,10 @@
 
 
 def grads_kernel(
-    nx, ny, inv, z, w_hbm, xt_hbm, st8, dxo, dwo, loss, rx, fx, dd, rr,
-    w, xt, zb, gb, acc, dx, st, lacc, tmpa, tmpb, keep, fin, fdx, lbuf,
+    nx, ny, inv, vocab, z, w_hbm, xt_hbm, sta_hbm, lab_hbm, dxo, dwo, loss, rx, fx, dd, rr,
+    w, xt, zb, gb, acc, dx, st, sta, laba, lacc, tmpa, tmpb, keep, fin, fdx, lbuf,
     wsem, tsem, zsem, xsend, xrecv, fsend, frecv, dsend, drecv, rsend, rrecv, osend, orecv, asem, bsem, lsend, lrecv,
-    out_sem,
+    out_sem, ssem,
 ):
     at = Place(nx, ny)
     x, y, c = at.x, at.y, at.c
@@ -454,7 +459,7 @@
     ch = zb.shape[2]
     sb = ch // TWO
     slot = NCH * sb
-    hk = dwo.shape[0]
+    hk = dwo.shape[1]
     nq = rx.shape[2]
     qr = tr // nq
     left, right = (x + nx - 1) % nx, (x + 1) % nx
@@ -465,8 +470,10 @@
     def adj(yy, b):
         return jnp.where((yy + b) % TWO == 0, (yy + ny - 1) % ny, (yy + 1) % ny)
 
-    for j in range(NCH):
-        local(w_hbm.at[j], w.at[j], wsem.at[j]).start()
+    stats = [local(sta_hbm, sta, ssem.at[0]), local(lab_hbm, laba, ssem.at[1])]
+    for cp in stats:
+        cp.start()
+    local(w_hbm.at[0], w.at[0], wsem.at[0]).start()
     barrier = pltpu.get_barrier_semaphore()
     for k in range(1, nx):
         pl.semaphore_signal(barrier, inc=1, device_id=at.dev(x=(x + k) % nx), device_id_type=MESH)
@@ -476,7 +483,6 @@
     pl.semaphore_signal(barrier, inc=1, device_id=at.dev(c=at.pc), device_id_type=MESH)
 
     segments = ["x0", "w0", "w1", "x1", "w2", "w3", "x2", "w4", "x3"]
-    segments += ["l%d" % j for j in range(NCH)]
     first, after, n_body = {}, {}, 0
     for seg in segments:
         first[seg] = n_body
@@ -487,7 +493,7 @@
         code, start = 0, 0
         for seg in segments[1:]:
             here = n >= first[seg]
-            code = jnp.where(here, "xwl".index(seg[0]) * 8 + int(seg[-1]), code)
+            code = jnp.where(here, int(seg.startswith("w")) * 8 + int(seg[-1]), code)
             start = jnp.where(here, first[seg], start)
         return code // 8, code % 8, n - start
 
@@ -504,13 +510,28 @@
 
     for u in BOTH:
         zcp(0, u, u).start()
+    for j in range(1, NCH):
+        local(w_hbm.at[j], w.at[j], wsem.at[j]).start()
     local(xt_hbm, xt, tsem).start()
 
-    def spread(run, _):
-        st[run] = jnp.concatenate([st8[run // nx, run % nx]] * 16, axis=0).T
-        return 0
-
-    lax.fori_loop(0, TWO * nx, spread, 0)
+    for cp in stats:
+        cp.wait()
+    for r in BOTH:
+        parts = [sta[sy, k, r] for sy in BOTH for k in range(nx)]
+        top = functools.reduce(jnp.maximum, [part[0:nx] for part in parts])
+        tot = sum(part[nx : TWO * nx] * jnp.exp(part[0:nx] - top) for part in parts)
+        shift = top + jnp.log(tot) - math.log(inv)
+        for d in range(nx):
+            col = jnp.full(laba.shape[TWO:], -1, jnp.int32)
+            for b in BOTH:
+                base = (x * TWO + b) * vocab + half_of(y, b, ny) * slot
+                pos = laba[r, d] - base
+                room = jnp.where(half_of(y, b, ny) == 0, slot, vocab - slot)
+                chunk = sum((pos >= q * sb).astype(jnp.int32) for q in range(1, NCH))
+                col = jnp.where((pos >= 0) & (pos < room), chunk * ch + b * sb + pos - chunk * sb, col)
+            line = jnp.concatenate([col[o : o + 1].astype(F32) for o in range(tr // LANES)], axis=1)
+            rows = jnp.concatenate([shift[d : d + 1], line, jnp.zeros((SUB - TWO, tr), F32)], axis=0)
+            st[r * nx + d] = jnp.concatenate([rows] * 16, axis=0).T
     lacc[...] = jnp.zeros_like(lacc)
     pl.semaphore_wait(barrier, nx - 1 + TWO * (ny - 1) + 1)
 
@@ -630,12 +651,12 @@
     def o_copy(j, b):
         kt = lot(b)[2]
         f = half_of(y, b, ny)
-        dst = dwo.at[:, pl.ds(pl.multiple_of(f * slot + j * sb, LANES), sb)]
+        dst = dwo.at[pl.ds(pl.multiple_of(f * slot + j * sb, SUB), sb)]
         return remote(fin.at[b], dst, osend.at[j, b], orecv.at[f, j], at.dev(y=kt, c=b))
 
     def o_here(j, b):
         f = half_of(y, b, ny)
-        dst = dwo.at[:, pl.ds(pl.multiple_of(f * slot + j * sb, LANES), sb)]
+        dst = dwo.at[pl.ds(pl.multiple_of(f * slot + j * sb, SUB), sb)]
         return local(fin.at[b], dst, orecv.at[f, j])
 
     def is_here(b):
@@ -653,7 +674,7 @@
             def _():
                 o_here(j - 1, b).wait()
 
-            fin[b] = (keep[j % TWO, b] + tmpb[b, 0]).astype(BF16)
+            fin[b] = (keep[j % TWO, b] + tmpb[b, 0]).T.astype(BF16)
 
             @pl.when(is_here(b))
             def _():
@@ -711,22 +732,14 @@
                 cols = slice(LANES * e, LANES * e + LANES)
                 fn(rows, cols, zb[buf, rows, cols] - shift, lane + float(LANES * e) == lab)
 
-    def make_g(n, u, buf, c0, c1):
+    def make_g(n, u, buf, c0, c1, loss_sum=None):
         def one(rows, cols, dist, hit):
             g = jnp.exp(dist)
             gb[u, rows, cols] = jnp.where(hit, g - inv, g).astype(BF16)
+            if loss_sum is not None:
+                loss_sum.append(jnp.where(hit, dist, 0.0) + (loss_sum.pop() if loss_sum else 0.0))
 
         each_tile(n, u, buf, c0, c1, one)
-
-    def l_body(n, base):
-        total = [jnp.zeros((SUB, LANES), F32)]
-
-        def one(rows, cols, dist, hit):
-            total[0] = total[0] + jnp.sum(jnp.where(hit, dist, 0.0).reshape(-1, SUB, LANES), axis=0)
-
-        for u in BOTH:
-            each_tile(n, u, base + u, 0, ch, one)
-        lacc[...] += total[0]
 
     big = ch % (10 * LANES) == 0
     x_cuts = [(ch * e // 5, ch * (e + 1) // 5) for e in range(5)] if big else [(0, ch)]
@@ -742,9 +755,11 @@
 
         for u in BOTH:
             for c0, c1 in x_cuts:
-                make_g(n, u, base + u, c0, c1)
+                loss_sum = []
+                make_g(n, u, base + u, c0, c1, loss_sum)
+                lacc[...] += jnp.sum(loss_sum[0].reshape(-1, SUB, LANES), axis=0)
                 dx[half, u] += lax.dot_general(
-                    gb[u, :, c0:c1], w[j, :, c0:c1], (((1,), (1,)), ((), ())), preferred_element_type=F32
+                    gb[u, :, c0:c1], w[j, c0:c1, :], (((1,), (0,)), ((), ())), preferred_element_type=F32
                 )
 
     def w_body(n, base):
@@ -762,15 +777,14 @@
                 xt[k], gb[:, :, c0:c1].reshape(TWO * tr, c1 - c0), preferred_element_type=F32
             )
 
-    late = after["x3"]
-    plan_a = [(after["x1"] + q, 1, q) for q in range(nq)] + [(after["x2"] + q, 2, q) for q in range(nq)]
-    plan_a += [(late + 1 + 7 * q - q // 3 * 2, 3, q) for q in range(nq)]
+    plan_a = [(after["x1"] + q, 1, q) for q in range(nq)]
+    plan_a += [(after["x2"] + q + q // 3 * 2, 2, q) for q in range(nq)] + [(n_body + q, 3, q) for q in range(nq)]
     plan_r = [(11, 12, 0), (15, 17, 1), (24, 25, 2), (28, 30, 3), (37, 38, 4)]
-    plan_s = [(18, 19, 0), (22, 23, 1), (31, 32, 2), (35, 36, 3), (late + 6, late + 7, 4)]
+    plan_s = [(18, 19, 0), (23, 24, 1), (31, 32, 2), (36, 37, 3), (n_body + 1, n_body + 2, 4)]
     pre_r, use_r = [(p, j) for p, _, j in plan_r], [(u, j) for _, u, j in plan_r]
     pre_s, use_s = [(p, j) for p, _, j in plan_s], [(u, j) for _, u, j in plan_s]
-    plan_f = [(late + 11, 0), (late + 18, 1), (n_body + TWO, 2), (n_body + 4, 3)]
-    n_all = n_body + 5
+    plan_f = [(n_body + nq + q, q) for q in range(nq)]
+    n_all = n_body + TWO * nq
 
     def when(n, table, fn):
         table = [(e[0], e[1:]) for e in table]
@@ -809,7 +823,7 @@
         when(n, pre_r, r_pre)
         when(n, pre_s, s_pre)
 
-        for at_n, fn in ((n_body, l_start), (n_body + TWO, l_mid), (n_body + 4, l_late)):
+        for at_n, fn in ((n_body, l_start), (n_body + TWO, l_mid), (n_body + nq, l_late)):
             pl.when(n == at_n)(fn)
 
         @pl.when((n == first["x2"]) | (n == first["x3"]))
@@ -848,10 +862,6 @@
             @pl.when(kind == 1)
             def _():
                 w_body(n, base)
-
-            @pl.when(kind == TWO)
-            def _():
-                l_body(n, base)
 
         return 0
 
@@ -885,7 +895,7 @@
         @pl.when(jnp.logical_not(kept))
         def _():
             for j in range(NCH):
-                dst = dwo.at[:, pl.ds(f * slot + j * sb, sb)]
+                dst = dwo.at[pl.ds(f * slot + j * sb, sb)]
                 remote(fin.at[0], dst, osend.at[j, 0], orecv.at[f, j], at.dev(c=at.pc)).wait_recv()
 
     for k in range(1, nx):
@@ -895,9 +905,8 @@
     l_copy(2, 0).wait_send()
 
 
-def grads(nx, ny, inv, z, w, xt, st8, hk):
-    h = w.shape[1]
-    ch = w.shape[2]
+def grads(nx, ny, inv, vocab, z, w, xt, sta, laba, hk):
+    ch, h = w.shape[1:]
     tr = z.shape[3]
     nq = 4
     shape = jax.ShapeDtypeStruct
@@ -906,28 +915,28 @@
     vspec = pl.BlockSpec(memory_space=pltpu.VMEM)
     sb, qr = ch // TWO, tr // nq
     return pl.pallas_call(
-        functools.partial(grads_kernel, nx, ny, inv),
+        functools.partial(grads_kernel, nx, ny, inv, vocab),
         out_shape=(
-            shape((tr, h), BF16), shape((hk, NCH * ch), BF16), shape((SUB, LANES), F32),
+            shape((tr, h), BF16), shape((NCH * ch, hk), BF16), shape((SUB, LANES), F32),
             shape((nx - 1, TWO, nq, qr, h), F32), shape((nq, qr, h), F32),
             shape((NCH, TWO, TWO, hk, sb), F32), shape((NCH, TWO, hk, sb), F32),
         ),
-        in_specs=[ANY, ANY, ANY, vspec],
+        in_specs=[ANY] * 5,
         out_specs=(ANY, ANY, vspec, ANY, ANY, ANY, ANY),
         scratch_shapes=[
-            vm((NCH, h, ch), BF16), vm((nx, h, TWO * tr), BF16), vm((4, tr, ch), F32), vm((TWO, tr, ch), BF16),
-            vm((TWO, h, ch), F32), vm((TWO, TWO, tr, h), F32), vm((TWO * nx, tr, LANES), F32), vm((SUB, LANES), F32),
+            vm((NCH, ch, h), BF16), vm((nx, h, TWO * tr), BF16), vm((4, tr, ch), F32), vm((TWO, tr, ch), BF16),
+            vm((TWO, h, ch), F32), vm((TWO, TWO, tr, h), F32), vm((TWO * nx, tr, LANES), F32), vm(sta.shape, F32), vm(laba.shape, jnp.int32), vm((SUB, LANES), F32),
             vm((TWO, TWO, qr, h), F32), vm((TWO, TWO, hk, sb), F32), vm((TWO, TWO, hk, sb), F32),
-            vm((TWO, hk, sb), BF16), vm((TWO, qr, h), BF16), vm((3, max(nx, ny), SUB, LANES), F32),
+            vm((TWO, sb, hk), BF16), vm((TWO, qr, h), BF16), vm((3, max(nx, ny), SUB, LANES), F32),
             dma((NCH,)), dma, dma((4,)), dma((nx - 1, TWO, nq)), dma((nx - 1, TWO, nq)), dma((nq,)), dma((nq,)),
             dma((NCH, TWO, TWO)), dma((NCH, TWO, TWO)), dma((NCH, TWO)), dma((NCH, TWO)), dma((NCH, TWO)), dma((TWO, NCH)),
-            dma((TWO, TWO)), dma((TWO, TWO)), dma((3, max(nx, ny))), dma((3, max(nx, ny))), dma((nq,)),
+            dma((TWO, TWO)), dma((TWO, TWO)), dma((3, max(nx, ny))), dma((3, max(nx, ny))), dma((nq,)), dma((TWO,)),
         ],
         compiler_params=pltpu.CompilerParams(
             collective_id=1, has_side_effects=True, vmem_limit_bytes=67_000_000
         ),
         name="grads",
-    )(z, w, xt, st8)
+    )(z, w, xt, sta, laba)
 
 
 def solution(mesh):
@@ -941,31 +950,11 @@
         tr, h = hidden.shape
         hk, vocab = w_head.shape
         inv = 1.0 / (tr * tp_size * ny)
-        vp = -(-vocab // (256 * NCH)) * (256 * NCH)
-        ch = vp // NCH
-        sb = ch // TWO
-        slot = NCH * sb
-        tp = lax.axis_index("tp")
-        x, y = tp // TWO, lax.axis_index("fsdp")
-        w_pad = jnp.pad(w_head, ((0, 0), (0, vp - vocab)))
-        lab8 = jnp.pad(labels.reshape(-1, LANES), ((0, SUB - tr // LANES), (0, 0)))
-        xg, wg, z, sta, laba, xt = gather_logits(nx, ny, vocab, hidden, w_pad, lab8)
-
-        ms = sta[..., 0, :].reshape(TWO * nx, TWO, nx, tr)
-        ss = sta[..., 1, :].reshape(TWO * nx, TWO, nx, tr)
-        top = jnp.max(ms, axis=0)
-        tot = jnp.sum(ss * jnp.exp(ms - top), axis=0)
-        lab = laba[:, :, 0 : tr // LANES, :].reshape(2, nx, tr)
-        shard, off = lab // vocab, lab % vocab
-        b, f = shard % TWO, off // slot
-        pos = off - f * slot
-        mine = (shard // TWO == x) & (half_of(y, b, ny) == f)
-        col = jnp.where(mine, (pos // sb) * ch + b * sb + pos % sb, -1)
-        rows = [top + jnp.log(tot) - jnp.log(inv), col.astype(F32)]
-        st8 = jnp.stack(rows + [jnp.zeros_like(top)] * 6, axis=2)
-        d_hidden, d_w, loss = grads(nx, ny, inv, z, wg, xt, st8, hk)[:3]
-        mean_loss = jnp.sum(loss) * inv + jnp.log(inv)
-        return mean_loss.reshape(1), d_hidden, d_w[:, :vocab]
+        lab = labels.reshape(-1, LANES)
+        xg, wg, z, sta, laba, xt = gather_logits(nx, ny, vocab, hidden, w_head.T, lab)
+        d_hidden, d_w, loss = grads(nx, ny, inv, vocab, z, wg, xt, sta, laba, hk)[:3]
+        mean_loss = jnp.sum(loss) * inv + math.log(inv)
+        return mean_loss.reshape(1), d_hidden, d_w[:vocab].T
 
     return jax.shard_map(
         local_step,

time: 409 us -> 384 us (0.939)
  the two profiles are of different devices: /device:TPU:97 before, /device:TPU:100 now
where the time goes in v4:
time: 384 us
  Pallas kernels  375 us (98%)
  local copies, waits for them, and re-layouts  4.78 us (1%)
    pallas_call x1, Pallas kernels, grads(): pl.pallas_call(functools.partial(grads_kernel, nx, ny, inv, vocab), out_s...  234 us
    pallas_call x1, Pallas kernels, gather_logits(): pl.pallas_call(functools.partial(gather_logits_kernel, nx, ny, vocab), ou...  142 us

profile of v4, /device:TPU:100, one launch (start us, length us, event | category | flops | bytes accessed | tf_op | source)
XLA Modules:
  0.0 383.9 jit_solution(5972032285322009168)
XLA Ops:
  0.6 141.8 %gather_logits.1 = (bf16[2,4,512,1024]{3,2,1,0:T(8,128)(2,1)}, bf16[5,1280,1024]{2,1,0:T(8,128)(2,1)}, f32[5,2,4,512,1280]{4,3,2,1,0:T(8,128)}, f32[2,4,2,8,512]...) custom-call(bf16[512,1024]{1,0:T(8,128)(2,1)} %x_hbm.1, bf16[6288,256]{1,0:T(8,128)(2,1)} %bitcast.5, ...), custom_call_target="tpu_custom_call" | custom-call | flops 53687091200 | bytes 104857600 | tf_op jit(solution)/shard_map/gather_logits/pallas_call | solution.py:422
  142.4 233.6 %grads.1 = (bf16[512,1024]{1,0:T(8,128)(2,1)}, bf16[6400,256]{1,0:T(8,128)(2,1)}, f32[8,128]{1,0:T(8,128)}, f32[3,2,4,128,1024]{4,3,2,1,0:T(8,128)}, f32[4,128,1...) custom-call(f32[5,2,4,512,1280]{4,3,2,1,0:T(8,128)} %get-tuple-element.11.z, ...), custom_call_target="tpu_custom_call" | custom-call | tf_op jit(solution)/shard_map/grads/pallas_call | solution.py:917
  376.0 0.0 copy-start
  376.0 1.4 reduce_sum.9
  378.0 3.8 slice_bitcast_fusion
  381.8 0.0 copy-done
  381.8 1.0 copy.7
Async XLA Ops:
  376.0 5.8 %copy-start = (bf16[512,1024]{1,0:T(8,128)(2,1)S(1)}, bf16[512,1024]{1,0:T(8,128)(2,1)}, u32[]{:S(2)}) copy-start(bf16[512,1024]{1,0:T(8,128)(2,1)} %get-tuple-element.23) | copy-start | bytes 3145732

commit v5 on v4

--- a/solution.py
+++ b/solution.py
@@ -136,6 +136,8 @@
         return remote(w_src(1 - at.half, q), w_dst(y, q), wsend.at[1, q], wrecv.at[1, q], at.dev(y=at.a))
 
     def w_far(q):
+        if q < TWO:
+            return remote(w_dst(at.a, q), w_dst(at.a, q), wsend.at[2, q], wrecv.at[2, q], at.dev(y=at.p))
         return remote(w_src(1 - at.half, q), w_dst(y, q), wsend.at[2, q], wrecv.at[2, q], at.dev(y=at.far))
 
     def w_core(q):
@@ -150,7 +152,8 @@
     def w_out(q):
         w_own(q).start()
         w_other(q).start()
-        w_far(q).start()
+        if q >= TWO:
+            w_far(q).start()
 
     x_send(0, RIGHT).start()
     x_send(0, LEFT).start()
@@ -160,9 +163,8 @@
             if rows_in(f, q) < sb:
                 pad = sb - rows_in(f, q)
                 wsrc[f * NCH + q, sb - pad :, :] = jnp.zeros((pad, hk), BF16)
-        w_out(q)
-        if q == 0:
-            x_far.start()
+        if q < TWO:
+            w_out(q)
     keep_x.start()
     for f, q in blocks:
         @pl.when(at.half == f)
@@ -201,6 +203,12 @@
             xtb.at[u], xt.at[run // TWO, :, pl.ds(pl.multiple_of((run % TWO) * tr, LANES), tr)], tsem.at[u]
         )
 
+    for q in BOTH:
+        w_other(q).wait_recv()
+        w_far(q).start()
+    x_far.start()
+    for q in range(TWO, NCH):
+        w_out(q)
     keep_x.wait()
     x_send(0, RIGHT).wait_recv()
     x_relay(0, RIGHT).start()
@@ -210,11 +218,10 @@
     n_steps = TWO * nx * NCH
 
     near = (0, 3, 1, 2)
-    order = [(0, k, 0) for k in near] + [(1, 0, 0)]
-    order += [(0, k, 1) for k in near] + [(1, 0, 1)]
-    order += [(1, k, j) for j in BOTH for k in (3, 1)]
-    order += [(0, k, 2) for k in near] + [(1, k, 2) for k in (0, 3, 1)] + [(1, 2, j) for j in range(3)]
-    order += [(r, k, j) for j in (3, 4) for r in BOTH for k in near]
+    order = [(0, k, j) for k in near for j in BOTH] + [(1, 0, 0), (1, 0, 1)]
+    order += [(0, k, 2) for k in near] + [(1, 0, 2), (1, 3, 0), (1, 3, 1), (1, 1, 0), (1, 1, 1), (1, 3, 2)]
+    order += [(0, k, 3) for k in near] + [(1, 1, 2)] + [(1, 2, j) for j in range(3)] + [(1, k, 3) for k in (0, 3, 1, 2)]
+    order += [(r, k, 4) for r in BOTH for k in near]
     codes = [(r * 4 + k) * 8 + j for r, k, j in order]
 
     def code_of(t):
@@ -290,42 +297,46 @@
             pl.when(at.half == f)(w_local(f, j).wait)
 
         w_own(j).wait_recv()
-        w_other(j).wait_recv()
+        if j >= TWO:
+            w_other(j).wait_recv()
         w_far(j).wait_recv()
         w_core(j).start()
 
-    here_at = (0, 2, 6, 11, 15)
-    both_at = (0, 2, 7, 12, 16)
+    here_at = (0, 0, 5, 9, 15)
+    both_at = (0, 0, 5, 10, 16)
 
     def body(t, held):
         older, old, now = held
         later = code_of(t + 1)
 
-        @pl.when(t == 0)
-        def _():
+        @pl.when((t == 0) | (t == 4) | (t == 7))
+        def _():
+            @pl.when(t == 4)
+            def _():
+                x_far.wait_recv()
+                x_send(1, RIGHT).start()
+                x_send(1, LEFT).start()
+
+            @pl.when(t == 7)
+            def _():
+                x_send(1, RIGHT).wait_recv()
+                x_relay(1, RIGHT).start()
+                x_send(1, LEFT).wait_recv()
+                x_relay(1, LEFT).start()
+
             for u in BOTH:
-                xcp(now[u], u).start()
-            x_relay(0, RIGHT).wait_recv()
-            x_relay(0, LEFT).wait_recv()
+                xcp(now[u], (t % TWO) * TWO + u).start()
 
         for j in range(NCH):
             pl.when(t == here_at[j])(functools.partial(w_here, j))
             pl.when(t == both_at[j])(w_core(j).wait_recv)
 
-        @pl.when(t == 1)
-        def _():
-            x_far.wait_recv()
-            x_send(1, RIGHT).start()
-            x_send(1, LEFT).start()
-
-        @pl.when(t == 4)
-        def _():
-            x_send(1, RIGHT).wait_recv()
-            x_relay(1, RIGHT).start()
-            x_send(1, LEFT).wait_recv()
-            x_relay(1, LEFT).start()
-
-        @pl.when(t == 9)
+        @pl.when(t == 2)
+        def _():
+            x_relay(0, RIGHT).wait_recv()
+            x_relay(0, LEFT).wait_recv()
+
+        @pl.when(t == 11)
         def _():
             x_relay(1, RIGHT).wait_recv()
             x_relay(1, LEFT).wait_recv()
@@ -351,7 +362,7 @@
                 xtb[u] = xb[base + u].T
                 cp.start()
 
-        @pl.when(TWO * t + 2 < n_steps)
+        @pl.when((TWO * t + 2 < n_steps) & (t != 3) & (t != 6))
         def _():
             for u in BOTH:
                 xcp(later[u], 2 - base + u).start()
@@ -482,7 +493,7 @@
         pl.semaphore_signal(barrier, inc=1, device_id=at.dev(y=(y + k) % ny, c=at.pc), device_id_type=MESH)
     pl.semaphore_signal(barrier, inc=1, device_id=at.dev(c=at.pc), device_id_type=MESH)
 
-    segments = ["x0", "w0", "w1", "x1", "w2", "w3", "x2", "w4", "x3"]
+    segments = ["x0", "w0", "w1", "x1", "w2", "w3", "x2", "x3", "w4"]
     first, after, n_body = {}, {}, 0
     for seg in segments:
         first[seg] = n_body
@@ -777,14 +788,14 @@
                 xt[k], gb[:, :, c0:c1].reshape(TWO * tr, c1 - c0), preferred_element_type=F32
             )
 
-    plan_a = [(after["x1"] + q, 1, q) for q in range(nq)]
-    plan_a += [(after["x2"] + q + q // 3 * 2, 2, q) for q in range(nq)] + [(n_body + q, 3, q) for q in range(nq)]
-    plan_r = [(11, 12, 0), (15, 17, 1), (24, 25, 2), (28, 30, 3), (37, 38, 4)]
-    plan_s = [(18, 19, 0), (23, 24, 1), (31, 32, 2), (36, 37, 3), (n_body + 1, n_body + 2, 4)]
+    plan_a = [(after["x1"] + q, 1, q) for q in range(nq)] + [(after["x2"] + q, 2, q) for q in range(nq)]
+    plan_a += [(after["x3"] + 3 * q, 3, q) for q in range(nq)]
+    plan_r = [(11, 12, 0), (15, 16, 1), (24, 25, 2), (28, 29, 3), (42, 43, 4)]
+    plan_s = [(17, 18, 0), (21, 22, 1), (30, 31, 2), (34, 35, 3), (46, 47, 4)]
     pre_r, use_r = [(p, j) for p, _, j in plan_r], [(u, j) for _, u, j in plan_r]
     pre_s, use_s = [(p, j) for p, _, j in plan_s], [(u, j) for _, u, j in plan_s]
-    plan_f = [(n_body + nq + q, q) for q in range(nq)]
-    n_all = n_body + TWO * nq
+    plan_f = [(41, 0), (44, 1), (46, 2), (48, 3)]
+    n_all = n_body + TWO * nq + 1
 
     def when(n, table, fn):
         table = [(e[0], e[1:]) for e in table]

time: 384 us -> 382 us (level)
  the two profiles are of different devices: /device:TPU:100 before, /device:TPU:97 now
where the time goes in v5:
time: 382 us
  Pallas kernels  373 us (98%)
  local copies, waits for them, and re-layouts  4.78 us (1%)
    pallas_call x1, Pallas kernels, grads(): pl.pallas_call(functools.partial(grads_kernel, nx, ny, inv, vocab), out_s...  211 us
    pallas_call x1, Pallas kernels, gather_logits(): pl.pallas_call(functools.partial(gather_logits_kernel, nx, ny, vocab), ou...  162 us

profile of v5, /device:TPU:97, one launch (start us, length us, event | category | flops | bytes accessed | tf_op | source)
XLA Modules:
  0.0 381.9 jit_solution(4198913743624939629)
XLA Ops:
  0.6 162.2 %gather_logits.1 = (bf16[2,4,512,1024]{3,2,1,0:T(8,128)(2,1)}, bf16[5,1280,1024]{2,1,0:T(8,128)(2,1)}, f32[5,2,4,512,1280]{4,3,2,1,0:T(8,128)}, f32[2,4,2,8,512]...) custom-call(bf16[512,1024]{1,0:T(8,128)(2,1)} %x_hbm.1, bf16[6288,256]{1,0:T(8,128)(2,1)} %bitcast.5, ...), custom_call_target="tpu_custom_call" | custom-call | flops 53687091200 | bytes 104857600 | tf_op jit(solution)/shard_map/gather_logits/pallas_call | solution.py:433
  162.9 211.0 %grads.1 = (bf16[512,1024]{1,0:T(8,128)(2,1)}, bf16[6400,256]{1,0:T(8,128)(2,1)}, f32[8,128]{1,0:T(8,128)}, f32[3,2,4,128,1024]{4,3,2,1,0:T(8,128)}, f32[4,128,1...) custom-call(f32[5,2,4,512,1280]{4,3,2,1,0:T(8,128)} %get-tuple-element.11.z, ...), custom_call_target="tpu_custom_call" | custom-call | tf_op jit(solution)/shard_map/grads/pallas_call | solution.py:928
  373.9 0.0 copy-start
  373.9 1.4 reduce_sum.9
  376.0 3.8 slice_bitcast_fusion
  379.8 0.0 copy-done
  379.8 1.0 copy.7
Async XLA Ops:
  373.9 5.8 %copy-start = (bf16[512,1024]{1,0:T(8,128)(2,1)S(1)}, bf16[512,1024]{1,0:T(8,128)(2,1)}, u32[]{:S(2)}) copy-start(bf16[512,1024]{1,0:T(8,128)(2,1)} %get-tuple-element.23) | copy-start | bytes 3145732

commit v6 on v4

--- a/solution.py
+++ b/solution.py
@@ -482,7 +482,7 @@
         pl.semaphore_signal(barrier, inc=1, device_id=at.dev(y=(y + k) % ny, c=at.pc), device_id_type=MESH)
     pl.semaphore_signal(barrier, inc=1, device_id=at.dev(c=at.pc), device_id_type=MESH)
 
-    segments = ["x0", "w0", "w1", "x1", "w2", "w3", "x2", "w4", "x3"]
+    segments = ["x0", "w0", "w1", "x1", "w2", "w3", "x2", "x3", "w4"]
     first, after, n_body = {}, {}, 0
     for seg in segments:
         first[seg] = n_body
@@ -777,14 +777,14 @@
                 xt[k], gb[:, :, c0:c1].reshape(TWO * tr, c1 - c0), preferred_element_type=F32
             )
 
-    plan_a = [(after["x1"] + q, 1, q) for q in range(nq)]
-    plan_a += [(after["x2"] + q + q // 3 * 2, 2, q) for q in range(nq)] + [(n_body + q, 3, q) for q in range(nq)]
-    plan_r = [(11, 12, 0), (15, 17, 1), (24, 25, 2), (28, 30, 3), (37, 38, 4)]
-    plan_s = [(18, 19, 0), (23, 24, 1), (31, 32, 2), (36, 37, 3), (n_body + 1, n_body + 2, 4)]
+    plan_a = [(after["x1"] + q, 1, q) for q in range(nq)] + [(after["x2"] + q, 2, q) for q in range(nq)]
+    plan_a += [(after["x3"] + 3 * q, 3, q) for q in range(nq)]
+    plan_r = [(11, 12, 0), (15, 16, 1), (24, 25, 2), (28, 29, 3), (42, 43, 4)]
+    plan_s = [(17, 18, 0), (21, 22, 1), (30, 31, 2), (34, 35, 3), (46, 47, 4)]
     pre_r, use_r = [(p, j) for p, _, j in plan_r], [(u, j) for _, u, j in plan_r]
     pre_s, use_s = [(p, j) for p, _, j in plan_s], [(u, j) for _, u, j in plan_s]
-    plan_f = [(n_body + nq + q, q) for q in range(nq)]
-    n_all = n_body + TWO * nq
+    plan_f = [(41, 0), (44, 1), (46, 2), (48, 3)]
+    n_all = n_body + TWO * nq + 1
 
     def when(n, table, fn):
         table = [(e[0], e[1:]) for e in table]

time: 384 us -> 365 us (0.951)
  the two profiles are of different devices: /device:TPU:100 before, /device:TPU:97 now
where the time goes in v6:
time: 365 us
  Pallas kernels  356 us (98%)
  local copies, waits for them, and re-layouts  4.78 us (1%)
    pallas_call x1, Pallas kernels, grads(): pl.pallas_call(functools.partial(grads_kernel, nx, ny, inv, vocab), out_s...  211 us
    pallas_call x1, Pallas kernels, gather_logits(): pl.pallas_call(functools.partial(gather_logits_kernel, nx, ny, vocab), ou...  145 us

profile of v6, /device:TPU:97, one launch (start us, length us, event | category | flops | bytes accessed | tf_op | source)
XLA Modules:
  0.0 364.7 jit_solution(1173446256718070673)
XLA Ops:
  0.6 145.3 %gather_logits.1 = (bf16[2,4,512,1024]{3,2,1,0:T(8,128)(2,1)}, bf16[5,1280,1024]{2,1,0:T(8,128)(2,1)}, f32[5,2,4,512,1280]{4,3,2,1,0:T(8,128)}, f32[2,4,2,8,512]...) custom-call(bf16[512,1024]{1,0:T(8,128)(2,1)} %x_hbm.1, bf16[6288,256]{1,0:T(8,128)(2,1)} %bitcast.5, ...), custom_call_target="tpu_custom_call" | custom-call | flops 53687091200 | bytes 104857600 | tf_op jit(solution)/shard_map/gather_logits/pallas_call | solution.py:422
  146.0 210.8 %grads.1 = (bf16[512,1024]{1,0:T(8,128)(2,1)}, bf16[6400,256]{1,0:T(8,128)(2,1)}, f32[8,128]{1,0:T(8,128)}, f32[3,2,4,128,1024]{4,3,2,1,0:T(8,128)}, f32[4,128,1...) custom-call(f32[5,2,4,512,1280]{4,3,2,1,0:T(8,128)} %get-tuple-element.11.z, ...), custom_call_target="tpu_custom_call" | custom-call | tf_op jit(solution)/shard_map/grads/pallas_call | solution.py:917
  356.7 0.0 copy-start
  356.8 1.4 reduce_sum.9
  358.8 3.8 %slice_bitcast_fusion = bf16[256,6288]{0,1:T(8,128)(2,1)} fusion(bf16[6400,256]{1,0:T(8,128)(2,1)} %get-tuple-element.18), kind=kLoop, calls=%fused_computation | loop fusion | bytes 6438912 | tf_op jit(solution)/shard_map/transpose | solution.py:957
  362.6 0.0 copy-done
  362.6 1.0 copy.7
Async XLA Ops:
  356.7 5.8 %copy-start = (bf16[512,1024]{1,0:T(8,128)(2,1)S(1)}, bf16[512,1024]{1,0:T(8,128)(2,1)}, u32[]{:S(2)}) copy-start(bf16[512,1024]{1,0:T(8,128)(2,1)} %get-tuple-element.23) | copy-start | bytes 3145732
